TPU v7x, 256 devices: a whole 4x4x8 slice. The times are simulated.
256 devices in a mesh: rows: 64 (over y, z, core), vocab: 4 (over x).
Axes of the slice: x: 4, y: 4, z: 8, core: 2. Of those that a mesh axis runs over, the one named last changes fastest.
Arguments:
- hidden_policy: bfloat16 [4096, 1536], P('rows', 'vocab'), may hold values from -45 to 45
- hidden_reference: bfloat16 [4096, 1536], P('rows', 'vocab'), may hold values from -45 to 45
- gain_policy: bfloat16 [1536], replicated, may hold values from 0.5 to 1.5
- gain_reference: bfloat16 [1536], replicated, may hold values from 0.5 to 1.5
- head_policy: bfloat16 [1536, 131072], P(None, ('rows', 'vocab')), may hold values from -20 to 20
- head_reference: bfloat16 [1536, 131072], P(None, ('rows', 'vocab')), may hold values from -20 to 20
- targets: int32 [4096], P('rows'), may hold values from 0 to 131071
- loss_mask: int32 [4096], P('rows'), may hold values from 0 to 1, as said below
- doc_lengths: int32 [128], replicated, may hold values from 1 to 127, as said below
- doc_owner: int32 [128], replicated, may hold values from 0 to 63, as said below
- doc_score: float32 [128], replicated, may hold values from -3 to 6
Outputs:
- token_logprob: float32 [8192], P('rows')
- doc_advantage: float32 [128], P('rows')
Inputs may be any that keep to these rules, and one draw needn't show every extreme that they name: `loss_mask`: each index of rows holds at most 32 ones among its 64 tokens, and some index holds exactly 32. `doc_lengths`: documents lie end to end in the pack in this order; their lengths add up to 4096. `doc_owner`: every index of rows owns exactly 2 documents, whose lengths add up to at most 128; for some index they add up to exactly 128.
All inputs are finite; a program needn't handle non-finite values.
Results may differ from a plain program's by a relative error of at most 0.0025.
Values may be sent and summed in bfloat16 or wider, within the bound.
No kernel may reach another device: no remote copies, remote signals or barrier semaphores. Data moves between devices by JAX's collectives and lax.ppermute only.
A program may use at most 128 MiB of HBM per device.

v0:
```python
import functools

import jax
import jax.numpy as jnp
from jax import lax
from jax.experimental import pallas as pl
from jax.experimental.pallas import tpu as pltpu
from jax.sharding import Mesh
from jax.sharding import PartitionSpec as P


DOC_DEV = 2
CAP = 128
LANES = 128
ROWS = ("y", "z", "c")
X = ("xh", "xl")
ALL = ("y", "z", "c", "xh", "xl")

epsilon = 1e-06
kl_weight = 0.1
f32 = jnp.float32
bf16 = jnp.bfloat16
VMEM = pl.BlockSpec(memory_space=pltpu.VMEM)
SMEM = pl.BlockSpec(memory_space=pltpu.SMEM)
ANY = pl.BlockSpec(memory_space=pl.ANY)


def iota(shape, dim):
    return lax.broadcasted_iota(jnp.int32, shape, dim)


def as_column(row):
    n = row.shape[1]
    return jnp.sum(jnp.where(iota((n, n), 0) == iota((n, n), 1), row, 0), axis=1, keepdims=True)


def pick_kernel(hp_ref, hr_ref, tgt_ref, mask_ref, out_ref):
    tok = hp_ref.shape[0]
    kept, half = tok // 2, tok // 4
    nz, nx, lines, _ = out_ref.shape
    per = (lines - 8) // half // 2
    mask_row = mask_ref[...]
    mask_col = as_column(mask_row)
    sub, lane = iota((tok, tok), 0), iota((tok, tok), 1)
    rank = jnp.sum(jnp.where(sub <= lane, mask_col, 0), axis=0, keepdims=True) - 1
    select = (iota((kept, tok), 0) == rank) & (mask_row == 1)
    one_hot = select.astype(f32).astype(bf16)
    target = jnp.sum(jnp.where(select, tgt_ref[...], 0), axis=1, keepdims=True)
    place = jnp.sum(
        jnp.where(select, iota((kept, tok), 1) + 1, 0), axis=1, keepdims=True
    )
    packed = [
        jnp.dot(one_hot, ref[...], preferred_element_type=f32).astype(bf16)
        for ref in (hp_ref, hr_ref)
    ]
    spot = iota((8, LANES), 1)
    for h in range(2):
        digits = jnp.zeros((8, LANES), jnp.int32)
        for g in range(2):
            part = slice(h * half + g * 8, h * half + g * 8 + 8)
            for k, value in enumerate(
                (target[part] & 63, (target[part] >> 6) & 63, target[part] >> 12, place[part])
            ):
                digits = jnp.where(spot == 4 * g + k, value, digits)
        digits = digits.astype(f32).astype(bf16)
        rows = slice(h * half, (h + 1) * half)
        pieces = [
            packed[m][rows, j * LANES : (j + 1) * LANES] for m in range(2) for j in range(per)
        ]
        for z in range(nz):
            for x in range(h, nx, 2):
                for t, piece in enumerate(pieces):
                    out_ref[z, x, t * half : (t + 1) * half] = piece
                out_ref[z, x, 2 * per * half :] = digits


def norm_kernel(in_ref, gp_ref, gr_ref, *out_refs):
    nz, nx, lines, _ = in_ref.shape
    half = 16
    per = (lines - 8) // half // 2
    width = nx * per * LANES
    share = nz // len(out_refs)
    for z in range(nz):
        out_ref, at = out_refs[z // share], z % share
        for m, gain_ref in enumerate((gp_ref, gr_ref)):
            parts = [
                in_ref[z, x, (m * per + j) * half : (m * per + j + 1) * half].astype(f32)
                for x in range(nx)
                for j in range(per)
            ]
            square = parts[0] * parts[0]
            for part in parts[1:]:
                square = square + part * part
            mean = jnp.sum(square, axis=1, keepdims=True) * (1.0 / width)
            inverse = lax.rsqrt(mean + epsilon)
            for k, part in enumerate(parts):
                gain = gain_ref[:, k * LANES : (k + 1) * LANES].astype(f32)
                t = m * nx * per + k
                out_ref[at, t * half : (t + 1) * half] = (part * inverse * gain).astype(bf16)
        out_ref[at, 2 * nx * per * half :] = in_ref[z, 0, 2 * per * half :]


def logits_kernel(base_ref, where_ref, *refs):
    toks, heads = refs[:8], refs[8:16]
    out_ref, lhs, held, even, odd, sem = refs[16:]
    copies = [pltpu.make_async_copy(heads[i], held.at[i], sem.at[i]) for i in range(8)]
    for copy in copies:
        copy.start()
    half = 16
    share, lines, _ = toks[0].shape
    per = (lines - 8) // half // 2
    nz = 2 * share
    ny = len(toks) // 2
    total = ny * nz * half
    columns = held.shape[2]
    target, place = [], []
    for y in range(ny):
        for z in range(nz):
            tok = toks[2 * y + z // share]
            at = z % share
            line = (y * nz + z) * half
            for m in range(2):
                for k in range(per):
                    t = m * per + k
                    lhs[m, line : line + half, k * LANES : (k + 1) * LANES] = tok[
                        at, t * half : (t + 1) * half
                    ]
            digit = tok[at, 2 * per * half :].astype(f32)
            for g in (0, 4):
                target.append(
                    digit[:, g : g + 1]
                    + 64.0 * digit[:, g + 1 : g + 2]
                    + 4096.0 * digit[:, g + 2 : g + 3]
                )
                place.append(digit[:, g + 3 : g + 4])
    target = jnp.concatenate(target, axis=0).astype(jnp.int32)
    place = jnp.concatenate(place, axis=0)
    column = iota((total, columns), 1)

    def product(i, out):
        for k in range(8):

            @pl.when(i == k)
            def _():
                copies[k].wait()

        out[...] = jnp.dot(lhs[i // 4], held[i], preferred_element_type=f32)

    def reduce(i, out, state):
        high, summed, hit = state
        values = out[...]
        fresh = lax.rem(i, 4) == 0
        here = jnp.max(values, axis=1, keepdims=True)
        old_high = jnp.where(fresh, here, high)
        new_high = jnp.maximum(old_high, here)
        part = jnp.sum(jnp.exp(values - new_high), axis=1, keepdims=True)
        summed = jnp.where(fresh, 0.0, summed) * jnp.exp(old_high - new_high) + part
        match = column == target - base_ref[i]
        hit = jnp.where(fresh, 0.0, hit) + jnp.sum(
            jnp.where(match, values, 0.0), axis=1, keepdims=True
        )
        return new_high, summed, hit

    def two(j, state):
        product(2 * j + 1, odd)
        state = reduce(2 * j, even, state)
        product(2 * j + 2, even)
        return reduce(2 * j + 1, odd, state)

    zero = jnp.zeros((total, 1), f32)
    product(0, even)
    policy = lax.fori_loop(0, 2, two, (zero, zero, zero))
    other = two(2, policy)
    product(7, odd)
    other = reduce(7, odd, reduce(6, even, other))
    row = nz * half
    diagonal = iota((row, LANES), 0) == iota((row, LANES), 1)
    for y in range(ny):
        to = where_ref[y]
        at = slice(y * row, (y + 1) * row)
        for v, value in enumerate(
            (
                policy[0] + jnp.log(policy[1]),
                policy[2],
                other[0] + jnp.log(other[1]),
                other[2],
                place,
            )
        ):
            line = jnp.sum(jnp.where(diagonal, value[at], 0.0), axis=0, keepdims=True)
            if v == 4:
                z = iota((1, LANES), 1) // half
                line = jnp.where(line > 0.0, line + (where_ref[4 + y] + 128 * z).astype(f32), 0.0)
            out_ref[pl.ds(4 * v + to, 1)] = line
    out_ref[20:24] = jnp.zeros((4, LANES), f32)


def total_of(lines):
    out = lines[0]
    for line in lines[1:]:
        out = out + line
    return out


def lse_of(lines):
    high = functools.reduce(jnp.maximum, lines)
    return high + jnp.log(total_of([jnp.exp(line - high) for line in lines]))


def merge_kernel(in_ref, out_ref):
    sources = in_ref.shape[0]
    for c in range(2):
        lines = [in_ref[s] for s in range(c, sources, 2)]
        lse, added = lse_of(lines), total_of(lines)
        for v in range(5):
            part = slice(4 * v, 4 * v + 4)
            value = (lse, added, lse, added, lines[0])[v]
            for k in range(out_ref.shape[0]):
                out_ref[k, v, 4 * c : 4 * c + 4] = value[part]


def as_row(column):
    n = column.shape[0]
    return jnp.sum(jnp.where(iota((n, n), 0) == iota((n, n), 1), column, 0), axis=0, keepdims=True)


def tables_kernel(me_ref, len_ref, owner_ref, score_ref, out_ref):
    me = me_ref[0]
    length, owner = len_ref[...], owner_ref[...]
    n = length.shape[1]
    sub, lane = iota((n, n), 0), iota((n, n), 1)
    length_col, owner_col = as_column(length), as_column(owner)
    earlier = lane < sub
    start = jnp.sum(jnp.where(earlier, length, 0), axis=1, keepdims=True)
    before = earlier & (owner_col == owner)
    offset = jnp.sum(jnp.where(before, length, 0), axis=1, keepdims=True)
    rank = jnp.sum(jnp.where(before, 1, 0), axis=1, keepdims=True)
    inside = (owner_col == me) & (lane >= offset) & (lane < offset + length_col)
    slot = jnp.sum(jnp.where(inside, start + lane - offset + 1, 0), axis=0, keepdims=True)
    slot = jnp.where(slot > 0, slot, -7)
    mine = owner_col == me
    table = jnp.zeros((n, n), f32)
    for k, value in enumerate(
        (
            start + 1,
            start + length_col + 1,
            as_column(slot),
            jnp.where(mine & (rank == 0), 1, 0),
            jnp.where(mine & (rank == 1), 1, 0),
        )
    ):
        table = jnp.where(lane == k, value.astype(f32), table)
    out_ref[...] = jnp.where(lane == 5, as_column(score_ref[...]), table)


def docs_kernel(in_ref, table_ref, token_ref, doc_ref):
    sources = in_ref.shape[0]
    table = table_ref[...]
    n = table.shape[0]
    low, high, slot, first, second, score = (table[:, k : k + 1] for k in range(6))
    count = jnp.zeros((n, LANES), f32)
    kl_sum, logprob = count, count
    for xl in range(2):
        lines = [[in_ref[s, v] for s in range(xl, sources, 2)] for v in range(5)]
        policy = total_of(lines[1]) - lse_of(lines[0])
        ratio = policy - (total_of(lines[3]) - lse_of(lines[2]))
        kl = 0.5 * ratio * ratio
        place = lines[4][0]
        for r in range(8):
            at = place[r : r + 1]
            within = (at >= low) & (at < high)
            count = count + jnp.where(within, 1.0, 0.0)
            kl_sum = kl_sum + jnp.where(within, kl[r : r + 1], 0.0)
            logprob = logprob + jnp.where(at == slot, policy[r : r + 1], 0.0)
    count = jnp.sum(count, axis=1, keepdims=True)
    kl_sum = jnp.sum(kl_sum, axis=1, keepdims=True)
    token_ref[...] = as_row(jnp.sum(logprob, axis=1, keepdims=True))
    reward = score - kl_weight * kl_sum / jnp.maximum(count, 1.0)
    baseline = jnp.sum(count * reward, axis=0, keepdims=True) / jnp.sum(
        count, axis=0, keepdims=True
    )
    advantage = reward - baseline
    doc_ref[:, 0:1] = jnp.sum(first * advantage, axis=0, keepdims=True)
    doc_ref[:, 1:2] = jnp.sum(second * advantage, axis=0, keepdims=True)


def shape_of(shape, dtype):
    return jax.ShapeDtypeStruct(shape, dtype)


def shifted(x, axis, by):
    n = lax.axis_size(axis)
    return lax.ppermute(x, axis, [(i, (i + by) % n) for i in range(n)])


def one_device(
    hidden_policy,
    hidden_reference,
    gain_policy,
    gain_reference,
    head_policy,
    head_reference,
    targets,
    loss_mask,
    doc_lengths,
    doc_owner,
    doc_score,
):
    ny, nz, nx = lax.axis_size("y"), lax.axis_size("z"), lax.axis_size(X)
    tok, width = hidden_policy.shape
    columns = head_policy.shape[1]
    per, half = width // LANES, tok // 4
    me, x = lax.axis_index(ROWS), lax.axis_index(X)
    c = lax.axis_index("c")

    pair_policy = [(i, i ^ 1) for i in range(nx)]
    pair_reference = [(i, (i + 1) % nx if i % 2 else (i - 1) % nx) for i in range(nx)]
    near_policy = lax.ppermute(head_policy, X, pair_policy)
    near_reference = lax.ppermute(head_reference, X, pair_reference)
    swapped = [shifted(near_policy, "c", 1), shifted(near_reference, "c", 1)]
    heads = [
        head_policy,
        shifted(head_policy, "c", 1),
        near_policy,
        swapped[0],
        head_reference,
        shifted(head_reference, "c", 1),
        near_reference,
        swapped[1],
    ]
    x_policy = x ^ 1
    x_reference = jnp.where(x % 2 == 1, (x + 1) % nx, (x + nx - 1) % nx)
    row_of = me - c
    bases = jnp.stack(
        [
            ((row_of + core) * nx + place) * columns
            for partner in (x_policy, x_reference)
            for place in (x, partner)
            for core in (c, 1 - c)
        ]
    ).astype(jnp.int32)

    lines = 2 * per * half + 8
    sent = pl.pallas_call(
        pick_kernel,
        out_shape=shape_of((nz, nx, lines, LANES), bf16),
        in_specs=[VMEM] * 4,
        out_specs=VMEM,
        name="pick",
    )(hidden_policy, hidden_reference, targets[None, :], loss_mask[None, :])
    got = lax.all_to_all(
        sent.reshape(nz * nx, lines, LANES), ("z", *X), 0, 0, tiled=True
    ).reshape(nz, nx, lines, LANES)
    wide = 2 * nx * per * half + 8
    own = pl.pallas_call(
        norm_kernel,
        out_shape=[shape_of((nz // 2, wide, LANES), bf16)] * 2,
        in_specs=[VMEM] * 3,
        out_specs=[VMEM] * 2,
        name="norm",
    )(got, gain_policy[None, :], gain_reference[None, :])
    below = [shifted(part, "y", 1) for part in own]
    above = [shifted(part, "y", -1) for part in own]
    far = [shifted(below[0], "y", 1), shifted(above[1], "y", -1)]
    lengths, _ = lax.optimization_barrier((doc_lengths, (below, above)))
    table = pl.pallas_call(
        tables_kernel,
        out_shape=shape_of((LANES, LANES), f32),
        in_specs=[SMEM] + [VMEM] * 3,
        out_specs=VMEM,
        name="tables",
    )(
        jnp.stack([me]).astype(jnp.int32),
        lengths[None, :],
        doc_owner[None, :],
        doc_score[None, :],
    )
    y = lax.axis_index("y")
    order = [y, (y + ny - 1) % ny, (y + 1) % ny, (y + 2) % ny]
    where = jnp.stack(order + [(row * nz * 2 + c) * tok for row in order]).astype(jnp.int32)
    total = ny * nz * half
    stats = pl.pallas_call(
        logits_kernel,
        out_shape=shape_of((24, LANES), f32),
        in_specs=[SMEM] * 2 + [VMEM] * 8 + [ANY] * 8,
        out_specs=VMEM,
        scratch_shapes=[
            pltpu.VMEM((2, total, nx * width), bf16),
            pltpu.VMEM((8, nx * width, columns), bf16),
            pltpu.VMEM((total, columns), f32),
            pltpu.VMEM((total, columns), f32),
            pltpu.SemaphoreType.DMA((8,)),
        ],
        compiler_params=pltpu.CompilerParams(vmem_limit_bytes=48 * 1024 * 1024),
        cost_estimate=pl.CostEstimate(
            flops=2 * 8 * total * nx * width * columns, bytes_accessed=1 << 24, transcendentals=0
        ),
        name="logits",
    )(bases, where, *own, *below, *above, *far, *heads)
    group = 2 * nz
    gathered = lax.all_to_all(
        jnp.broadcast_to(stats[None], (group, *stats.shape)), ("z", "c"), 0, 0, tiled=True
    )
    group = ny * nx
    merged = pl.pallas_call(
        merge_kernel,
        out_shape=shape_of((group, 5, 8, LANES), f32),
        in_specs=[VMEM],
        out_specs=VMEM,
        name="merge",
    )(gathered)
    everything = lax.all_to_all(merged, ("y", *X), 0, 0, tiled=True)
    token_logprob, advantage = pl.pallas_call(
        docs_kernel,
        out_shape=(shape_of((1, CAP), f32), shape_of((1, DOC_DEV), f32)),
        in_specs=[VMEM] * 2,
        out_specs=(VMEM, VMEM),
        name="docs",
    )(everything, table)
    return token_logprob.reshape(CAP), advantage.reshape(DOC_DEV)


def solution(mesh):
    finer = Mesh(
        mesh.devices.reshape(4, 8, 2, 2, mesh.shape["vocab"] // 2), ("y", "z", "c", "xh", "xl")
    )
    placed = (
        P(ROWS, X),
        P(ROWS, X),
        P(),
        P(),
        P(None, ALL),
        P(None, ALL),
        P(ROWS),
        P(ROWS),
        P(),
        P(),
        P(),
    )
    return jax.shard_map(
        one_device, mesh=finer, in_specs=placed, out_specs=(P(ROWS), P(ROWS)), check_vma=False
    )
```

profile of v0, /device:TPU:1, one launch (start us, length us, event | category | flops | bytes accessed | tf_op | source)
XLA Modules:
  0.0 136.7 jit_solution(14535059696483059246)
XLA Ops:
  0.6 0.0 copy-start
  0.6 0.0 copy-start.5
  0.7 0.0 copy-start.6
  0.7 3.4 %collective-permute-start.10 = (bf16[1536,512]{1,0:T(8,128)(2,1)}, bf16[1536,512]{1,0:T(8,128)(2,1)}, u32[]{:S(2)}, u32[]{:S(2)}) collective-permute-start(bf16[1536,512]{1,0:T(8,128)(2,1)} %refs_12_.1), channel_id=1, source_target_pairs={{0,3},{1,2},{2,1},{3,0},{4,7},{5,6},{6,5},{7,4},{8,11},{9,10},{10,... | collective-permute-start | bytes 4718600 | tf_op jit(solution)/shard_map/ppermute | solution.py:319
  4.0 0.0 collective-permute-start.7
  4.0 2.0 %pick.1 = bf16[8,4,104,128]{3,2,1,0:T(8,128)(2,1)} custom-call(bf16[64,384]{1,0:T(8,128)(2,1)} %hp_ref.1, bf16[64,384]{1,0:T(8,128)(2,1)} %hr_ref.1, s32[1,64]{1,0:T(1,128)} %bitcast.26, s32[1,64]{1,0:T(1,128)} %bitcast.27), custom_call_target="tpu_custom_call" | custom-call | tf_op jit(solution)/shard_map/pick/pallas_call | solution.py:344
  6.1 9.8 %all-to-all-start = ((bf16[32,104,128]{2,1,0:T(8,128)(2,1)}), bf16[32,104,128]{2,1,0:T(8,128)(2,1)S(1)}, u32[]{:S(2)}, u32[]{:S(2)}) async-start(bf16[32,104,128]{2,1,0:T(8,128)(2,1)} %bitcast.25), calls=%async_computation | async-start | bytes 1703936 | tf_op jit(solution)/shard_map/all_to_all | solution.py:351
  15.8 0.0 copy-done
  15.8 1.6 %collective-permute-start.6 = (bf16[1536,512]{1,0:T(8,128)(2,1)S(1)}, bf16[1536,512]{1,0:T(8,128)(2,1)}, u32[]{:S(2)}, u32[]{:S(2)}) collective-permute-start(bf16[1536,512]{1,0:T(8,128)(2,1)S(1)} %copy-done), channel_id=1, source_target_pairs={{0,4},{4,0},{1,5},{5,1},{2,6},{6,2},{3,7},{7,3},{8,12},{12,8},{9,1... | collective-permute-start | bytes 4718600 | tf_op jit(solution)/shard_map/ppermute | solution.py:293
  17.4 0.1 collective-permute-start.9
  17.5 27.9 %collective-permute-done.10.refs_14_ = bf16[1536,512]{1,0:T(8,128)(2,1)} collective-permute-done((bf16[1536,512]{1,0:T(8,128)(2,1)}, bf16[1536,512]{1,0:T(8,128)(2,1)}, u32[]{:S(2)}, u32[]{:S(2)}) %collective-permute-start.10) | collective-permute-done | bytes 1572896 | tf_op jit(solution)/shard_map/ppermute | solution.py:319
  45.4 2.8 %collective-permute-start.11 = (bf16[1536,512]{1,0:T(8,128)(2,1)}, bf16[1536,512]{1,0:T(8,128)(2,1)}, u32[]{:S(2)}, u32[]{:S(2)}) collective-permute-start(bf16[1536,512]{1,0:T(8,128)(2,1)} %collective-permute-done.10.refs_14_), channel_id=1, source_target_pairs={{0,4},{4,0},{1,5},{5,1},{2,6},{6,2},{3,7},{7,3},{8,12},{12,8},{9,1... | collective-permute-start | bytes 4718600 | tf_op jit(solution)/shard_map/ppermute | solution.py:293
  48.3 0.0 collective-permute-done.7.refs_10_
  48.3 1.5 %collective-permute-start.8 = (bf16[1536,512]{1,0:T(8,128)(2,1)}, bf16[1536,512]{1,0:T(8,128)(2,1)}, u32[]{:S(2)}, u32[]{:S(2)}) collective-permute-start(bf16[1536,512]{1,0:T(8,128)(2,1)} %collective-permute-done.7.refs_10_), channel_id=1, source_target_pairs={{0,4},{4,0},{1,5},{5,1},{2,6},{6,2},{3,7},{7,3},{8,12},{12,8},{9,1... | collective-permute-start | bytes 4718600 | tf_op jit(solution)/shard_map/ppermute | solution.py:293
  49.7 0.0 copy-done.5
  49.7 0.6 broadcast_in_dim.29.gp_ref
  50.3 0.0 copy-done.6
  50.3 0.6 broadcast_in_dim.30.gr_ref
  50.9 0.0 all-to-all-done
  50.9 0.0 copy-start.3
  50.9 0.9 copy-done.3
  51.8 2.4 %norm.1 = (bf16[4,392,128]{2,1,0:T(8,128)(2,1)}, bf16[4,392,128]{2,1,0:T(8,128)(2,1)}) custom-call(bf16[8,4,104,128]{3,2,1,0:T(8,128)(2,1)} %bitcast.24, bf16[1,1536]{1,0:T(2,128)(2,1)} %broadcast_in_dim.29.gp_ref, bf16[1,1536]{1,0:T(2,128)(2,1)} %broadcast_in_dim.30.gr_ref), custom_call_target="tpu_custom_call" | custom-call | tf_op jit(solution)/shard_map/norm/pallas_call | solution.py:355
  54.2 1.3 collective-permute-start
  55.5 0.0 collective-permute-done.6.refs_9_
  55.5 1.5 %collective-permute-start.3 = (bf16[4,392,128]{2,1,0:T(8,128)(2,1)}, bf16[4,392,128]{2,1,0:T(8,128)(2,1)S(1)}, u32[]{:S(2)}, u32[]{:S(2)}) collective-permute-start(bf16[4,392,128]{2,1,0:T(8,128)(2,1)} %get-tuple-element.8.refs_1_), channel_id=1, source_target_pairs={{0,192},{64,0},{128,64},{192,128},{1,193},{65,1},{129,65},{193,129... | collective-permute-start | bytes 1204232 | tf_op jit(solution)/shard_map/ppermute | solution.py:293
  57.0 0.0 collective-permute-done.9.refs_13_
  57.0 0.0 collective-permute-start.1
  57.0 9.6 %collective-permute-done.refs_2_ = bf16[4,392,128]{2,1,0:T(8,128)(2,1)S(1)} collective-permute-done((bf16[4,392,128]{2,1,0:T(8,128)(2,1)}, bf16[4,392,128]{2,1,0:T(8,128)(2,1)S(1)}, u32[]{:S(2)}, u32[]{:S(2)}) %collective-permute-start) | collective-permute-done | bytes 401440 | tf_op jit(solution)/shard_map/ppermute | solution.py:293
  66.6 1.4 %collective-permute-start.2 = (bf16[4,392,128]{2,1,0:T(8,128)(2,1)}, bf16[4,392,128]{2,1,0:T(8,128)(2,1)S(1)}, u32[]{:S(2)}, u32[]{:S(2)}) collective-permute-start(bf16[4,392,128]{2,1,0:T(8,128)(2,1)} %get-tuple-element.7.refs_0_), channel_id=1, source_target_pairs={{0,192},{64,0},{128,64},{192,128},{1,193},{65,1},{129,65},{193,129... | collective-permute-start | bytes 1204232 | tf_op jit(solution)/shard_map/ppermute | solution.py:293
  68.0 0.0 collective-permute-done.3.refs_5_
  68.0 0.1 collective-permute-start.4
  68.0 7.1 %collective-permute-done.1.refs_3_ = bf16[4,392,128]{2,1,0:T(8,128)(2,1)S(1)} collective-permute-done((bf16[4,392,128]{2,1,0:T(8,128)(2,1)}, bf16[4,392,128]{2,1,0:T(8,128)(2,1)S(1)}, u32[]{:S(2)}, u32[]{:S(2)}) %collective-permute-start.1) | collective-permute-done | bytes 401440 | tf_op jit(solution)/shard_map/ppermute | solution.py:293
  75.2 1.4 %collective-permute-start.5 = (bf16[4,392,128]{2,1,0:T(8,128)(2,1)S(1)}, bf16[4,392,128]{2,1,0:T(8,128)(2,1)}, u32[]{:S(2)}, u32[]{:S(2)}) collective-permute-start(bf16[4,392,128]{2,1,0:T(8,128)(2,1)S(1)} %collective-permute-done.3.refs_5_), channel_id=1, source_target_pairs={{0,192},{64,0},{128,64},{192,128},{1,193},{65,1},{129,65},{193,129... | collective-permute-start | bytes 1204232 | tf_op jit(solution)/shard_map/ppermute | solution.py:293
  76.6 0.1 stack.59.base_ref
  76.7 0.1 stack.68.where_ref
  76.8 0.0 collective-permute-done.2.refs_4_
  76.8 7.1 %collective-permute-done.4.refs_6_ = bf16[4,392,128]{2,1,0:T(8,128)(2,1)} collective-permute-done((bf16[4,392,128]{2,1,0:T(8,128)(2,1)S(1)}, bf16[4,392,128]{2,1,0:T(8,128)(2,1)}, u32[]{:S(2)}, u32[]{:S(2)}) %collective-permute-start.4) | collective-permute-done | bytes 401440 | tf_op jit(solution)/shard_map/ppermute | solution.py:293
  83.9 1.5 %collective-permute-done.5.refs_7_ = bf16[4,392,128]{2,1,0:T(8,128)(2,1)} collective-permute-done((bf16[4,392,128]{2,1,0:T(8,128)(2,1)S(1)}, bf16[4,392,128]{2,1,0:T(8,128)(2,1)}, u32[]{:S(2)}, u32[]{:S(2)}) %collective-permute-start.5) | collective-permute-done | bytes 401440 | tf_op jit(solution)/shard_map/ppermute | solution.py:293
  85.4 0.0 collective-permute-done.11.refs_15_
  85.4 0.0 collective-permute-done.8.refs_11_
  85.4 0.0 copy-start.1
  85.4 1.0 copy-done.1
  86.4 0.0 copy-start.2
  86.4 1.0 copy-done.2
  87.4 10.7 %logits.1 = f32[24,128]{1,0:T(8,128)S(1)} custom-call(s32[8]{0:T(128)S(1)} %stack.59.base_ref, s32[8]{0:T(128)S(1)} %stack.68.where_ref, bf16[4,392,128]{2,1,0:T(8,128)(2,1)S(1)} %copy-done.1, bf16[4,392,128]{2,1,0:T(8,128)(2,1)S(1)} %copy-done.2, bf16[4,392,128]{2,1,0:T(8,128)(2,1)S(1)} %collective-permute-done.refs_2_, ...), custom_call_target="tpu_custom_call" | custom-call | flops 6442450944 | bytes 16777216 | tf_op jit(solution)/shard_map/logits/pallas_call | solution.py:382
  98.1 20.4 %all_to_all.15.in_ref = f32[16,24,128]{2,1,0:T(8,128)} all-to-all(f32[16,24,128]{2,1,0:T(8,128)S(1)} %broadcast_in_dim.31), channel_id=1, replica_groups=mesh['y'=4,'z'=8,'c'=2,'xh'=2,'xl'=2] {'z','c'}, dimensions={0} | all-to-all | bytes 393216 | tf_op jit(solution)/shard_map/all_to_all | solution.py:401
  118.5 1.7 %merge.1 = f32[16,5,8,128]{3,2,1,0:T(8,128)} custom-call(f32[16,24,128]{2,1,0:T(8,128)} %all_to_all.15.in_ref), custom_call_target="tpu_custom_call" | custom-call | tf_op jit(solution)/shard_map/merge/pallas_call | solution.py:405
  120.2 4.4 %all-to-all-start.2 = ((f32[16,5,8,128]{3,2,1,0:T(8,128)}), f32[16,5,8,128]{3,2,1,0:T(8,128)S(1)}, u32[]{:S(2)}, u32[]{:S(2)}) async-start(f32[16,5,8,128]{3,2,1,0:T(8,128)} %merge.1), calls=%async_computation.2 | async-start | bytes 655360 | tf_op jit(solution)/shard_map/all_to_all | solution.py:412
  124.7 1.7 %tables.1.table_ref = f32[128,128]{1,0:T(8,128)} custom-call(s32[1]{0:T(128)} %bitcast.18.me_ref, s32[1,128]{1,0:T(1,128)} %bitcast.28, s32[1,128]{1,0:T(1,128)} %bitcast.29, f32[1,128]{1,0:T(1,128)} %bitcast.30), custom_call_target="tpu_custom_call" | custom-call | tf_op jit(solution)/shard_map/tables/pallas_call | solution.py:366
  126.3 7.4 %all-to-all-done.2.in_ref = f32[16,5,8,128]{3,2,1,0:T(8,128)S(1)} async-done(((f32[16,5,8,128]{3,2,1,0:T(8,128)}), f32[16,5,8,128]{3,2,1,0:T(8,128)S(1)}, u32[]{:S(2)}, u32[]{:S(2)}) %all-to-all-start.2) | async-done | bytes 327712 | tf_op jit(solution)/shard_map/all_to_all | solution.py:412
  133.8 0.0 copy-start.4
  133.8 0.7 copy-done.4
  134.5 2.1 %docs.1 = (f32[1,128]{1,0:T(1,128)}, f32[1,2]{1,0:T(1,128)}) custom-call(f32[16,5,8,128]{3,2,1,0:T(8,128)} %copy-done.4, f32[128,128]{1,0:T(8,128)} %tables.1.table_ref), custom_call_target="tpu_custom_call" | custom-call | tf_op jit(solution)/shard_map/docs/pallas_call | solution.py:413
  (1 shorter events, 0.0 us)
Async XLA Ops:
  0.6 15.2 %copy-start = (bf16[1536,512]{1,0:T(8,128)(2,1)S(1)}, bf16[1536,512]{1,0:T(8,128)(2,1)}, u32[]{:S(2)}) copy-start(bf16[1536,512]{1,0:T(8,128)(2,1)} %refs_8_.1) | copy-start | bytes 4718596
  0.6 49.1 %copy-start.5 = (bf16[1536]{0:T(1024)(128)(2,1)S(1)}, bf16[1536]{0:T(1024)(128)(2,1)}, u32[]{:S(2)}) copy-start(bf16[1536]{0:T(1024)(128)(2,1)} %param.13) | copy-start | bytes 9220
  0.7 49.7 %copy-start.6 = (bf16[1536]{0:T(1024)(128)(2,1)S(1)}, bf16[1536]{0:T(1024)(128)(2,1)}, u32[]{:S(2)}) copy-start(bf16[1536]{0:T(1024)(128)(2,1)} %param.14) | copy-start | bytes 9220
  0.7 44.8 %collective-permute-start.10 = (bf16[1536,512]{1,0:T(8,128)(2,1)}, bf16[1536,512]{1,0:T(8,128)(2,1)}, u32[]{:S(2)}, u32[]{:S(2)}) collective-permute-start(bf16[1536,512]{1,0:T(8,128)(2,1)} %refs_12_.1), channel_id=1, source_target_pairs={{0,3},{1,2},{2,1},{3,0},{4,7},{5,6},{6,5},{7,4},{8,11},{9,10},{10,... | collective-permute-start | bytes 4718600 | tf_op jit(solution)/shard_map/ppermute | solution.py:319
  4.0 44.2 %collective-permute-start.7 = (bf16[1536,512]{1,0:T(8,128)(2,1)}, bf16[1536,512]{1,0:T(8,128)(2,1)}, u32[]{:S(2)}, u32[]{:S(2)}) collective-permute-start(bf16[1536,512]{1,0:T(8,128)(2,1)} %refs_8_.1), channel_id=1, source_target_pairs={{0,1},{1,0},{2,3},{3,2},{4,5},{5,4},{6,7},{7,6},{8,9},{9,8},{10,11... | collective-permute-start | bytes 4718600 | tf_op jit(solution)/shard_map/ppermute | solution.py:318
  6.1 44.9 %all-to-all-start = ((bf16[32,104,128]{2,1,0:T(8,128)(2,1)}), bf16[32,104,128]{2,1,0:T(8,128)(2,1)S(1)}, u32[]{:S(2)}, u32[]{:S(2)}) async-start(bf16[32,104,128]{2,1,0:T(8,128)(2,1)} %bitcast.25), calls=%async_computation | async-start | bytes 1703936 | tf_op jit(solution)/shard_map/all_to_all | solution.py:351
  15.8 39.7 %collective-permute-start.6 = (bf16[1536,512]{1,0:T(8,128)(2,1)S(1)}, bf16[1536,512]{1,0:T(8,128)(2,1)}, u32[]{:S(2)}, u32[]{:S(2)}) collective-permute-start(bf16[1536,512]{1,0:T(8,128)(2,1)S(1)} %copy-done), channel_id=1, source_target_pairs={{0,4},{4,0},{1,5},{5,1},{2,6},{6,2},{3,7},{7,3},{8,12},{12,8},{9,1... | collective-permute-start | bytes 4718600 | tf_op jit(solution)/shard_map/ppermute | solution.py:293
  17.4 39.6 %collective-permute-start.9 = (bf16[1536,512]{1,0:T(8,128)(2,1)}, bf16[1536,512]{1,0:T(8,128)(2,1)}, u32[]{:S(2)}, u32[]{:S(2)}) collective-permute-start(bf16[1536,512]{1,0:T(8,128)(2,1)} %refs_12_.1), channel_id=1, source_target_pairs={{0,4},{4,0},{1,5},{5,1},{2,6},{6,2},{3,7},{7,3},{8,12},{12,8},{9,1... | collective-permute-start | bytes 4718600 | tf_op jit(solution)/shard_map/ppermute | solution.py:293
  45.4 39.9 %collective-permute-start.11 = (bf16[1536,512]{1,0:T(8,128)(2,1)}, bf16[1536,512]{1,0:T(8,128)(2,1)}, u32[]{:S(2)}, u32[]{:S(2)}) collective-permute-start(bf16[1536,512]{1,0:T(8,128)(2,1)} %collective-permute-done.10.refs_14_), channel_id=1, source_target_pairs={{0,4},{4,0},{1,5},{5,1},{2,6},{6,2},{3,7},{7,3},{8,12},{12,8},{9,1... | collective-permute-start | bytes 4718600 | tf_op jit(solution)/shard_map/ppermute | solution.py:293
  48.3 37.1 %collective-permute-start.8 = (bf16[1536,512]{1,0:T(8,128)(2,1)}, bf16[1536,512]{1,0:T(8,128)(2,1)}, u32[]{:S(2)}, u32[]{:S(2)}) collective-permute-start(bf16[1536,512]{1,0:T(8,128)(2,1)} %collective-permute-done.7.refs_10_), channel_id=1, source_target_pairs={{0,4},{4,0},{1,5},{5,1},{2,6},{6,2},{3,7},{7,3},{8,12},{12,8},{9,1... | collective-permute-start | bytes 4718600 | tf_op jit(solution)/shard_map/ppermute | solution.py:293
  50.9 0.9 copy-start.3
  54.2 12.4 %collective-permute-start = (bf16[4,392,128]{2,1,0:T(8,128)(2,1)}, bf16[4,392,128]{2,1,0:T(8,128)(2,1)S(1)}, u32[]{:S(2)}, u32[]{:S(2)}) collective-permute-start(bf16[4,392,128]{2,1,0:T(8,128)(2,1)} %get-tuple-element.7.refs_0_), channel_id=1, source_target_pairs={{0,64},{64,128},{128,192},{192,0},{1,65},{65,129},{129,193},{193,1... | collective-permute-start | bytes 1204232 | tf_op jit(solution)/shard_map/ppermute | solution.py:293
  55.5 12.5 %collective-permute-start.3 = (bf16[4,392,128]{2,1,0:T(8,128)(2,1)}, bf16[4,392,128]{2,1,0:T(8,128)(2,1)S(1)}, u32[]{:S(2)}, u32[]{:S(2)}) collective-permute-start(bf16[4,392,128]{2,1,0:T(8,128)(2,1)} %get-tuple-element.8.refs_1_), channel_id=1, source_target_pairs={{0,192},{64,0},{128,64},{192,128},{1,193},{65,1},{129,65},{193,129... | collective-permute-start | bytes 1204232 | tf_op jit(solution)/shard_map/ppermute | solution.py:293
  57.0 18.2 %collective-permute-start.1 = (bf16[4,392,128]{2,1,0:T(8,128)(2,1)}, bf16[4,392,128]{2,1,0:T(8,128)(2,1)S(1)}, u32[]{:S(2)}, u32[]{:S(2)}) collective-permute-start(bf16[4,392,128]{2,1,0:T(8,128)(2,1)} %get-tuple-element.8.refs_1_), channel_id=1, source_target_pairs={{0,64},{64,128},{128,192},{192,0},{1,65},{65,129},{129,193},{193,1... | collective-permute-start | bytes 1204232 | tf_op jit(solution)/shard_map/ppermute | solution.py:293
  66.6 10.2 %collective-permute-start.2 = (bf16[4,392,128]{2,1,0:T(8,128)(2,1)}, bf16[4,392,128]{2,1,0:T(8,128)(2,1)S(1)}, u32[]{:S(2)}, u32[]{:S(2)}) collective-permute-start(bf16[4,392,128]{2,1,0:T(8,128)(2,1)} %get-tuple-element.7.refs_0_), channel_id=1, source_target_pairs={{0,192},{64,0},{128,64},{192,128},{1,193},{65,1},{129,65},{193,129... | collective-permute-start | bytes 1204232 | tf_op jit(solution)/shard_map/ppermute | solution.py:293
  68.0 15.9 %collective-permute-start.4 = (bf16[4,392,128]{2,1,0:T(8,128)(2,1)S(1)}, bf16[4,392,128]{2,1,0:T(8,128)(2,1)}, u32[]{:S(2)}, u32[]{:S(2)}) collective-permute-start(bf16[4,392,128]{2,1,0:T(8,128)(2,1)S(1)} %collective-permute-done.refs_2_), channel_id=1, source_target_pairs={{0,64},{64,128},{128,192},{192,0},{1,65},{65,129},{129,193},{193,1... | collective-permute-start | bytes 1204232 | tf_op jit(solution)/shard_map/ppermute | solution.py:293
  75.2 10.2 %collective-permute-start.5 = (bf16[4,392,128]{2,1,0:T(8,128)(2,1)S(1)}, bf16[4,392,128]{2,1,0:T(8,128)(2,1)}, u32[]{:S(2)}, u32[]{:S(2)}) collective-permute-start(bf16[4,392,128]{2,1,0:T(8,128)(2,1)S(1)} %collective-permute-done.3.refs_5_), channel_id=1, source_target_pairs={{0,192},{64,0},{128,64},{192,128},{1,193},{65,1},{129,65},{193,129... | collective-permute-start | bytes 1204232 | tf_op jit(solution)/shard_map/ppermute | solution.py:293
  85.4 1.0 copy-start.1
  86.4 1.0 copy-start.2
  120.2 13.5 %all-to-all-start.2 = ((f32[16,5,8,128]{3,2,1,0:T(8,128)}), f32[16,5,8,128]{3,2,1,0:T(8,128)S(1)}, u32[]{:S(2)}, u32[]{:S(2)}) async-start(f32[16,5,8,128]{3,2,1,0:T(8,128)} %merge.1), calls=%async_computation.2 | async-start | bytes 655360 | tf_op jit(solution)/shard_map/all_to_all | solution.py:412
  133.8 0.7 copy-start.4
where the time goes:
time: 137 us
  waiting for transfers between devices  60.6 us (44%)
  starting transfers between devices  29.2 us (21%)
  Pallas kernels  20.6 us (15%)
  blocking collectives  20.4 us (15%)
  local copies, waits for them, and re-layouts  5.02 us (4%)
    ppermute x1, waiting for transfers between devices, one_device(): near_reference = lax.ppermute(head_reference, X, pair_reference)  27.9 us
    ppermute x10, waiting for transfers between devices, shifted(): return lax.ppermute(x, axis, [(i, (i + by) % n) for i in range(n)])  25.3 us
    all_to_all x1, blocking collectives, one_device(): lax.all_to_all(jnp.broadcast_to(stats[None], (group, *stats.shape)), ('z'...  20.4 us
    ppermute x10, starting transfers between devices, shifted(): return lax.ppermute(x, axis, [(i, (i + by) % n) for i in range(n)])  11.7 us
    pallas_call x1, Pallas kernels, one_device(): pl.pallas_call(logits_kernel, out_shape=shape_of((24, LANES), f32), in_sp...  10.7 us
    all_to_all x1, starting transfers between devices, one_device(): lax.all_to_all(sent.reshape(nz * nx, lines, LANES), ('z', *X), 0, 0, tile...  9.75 us
    all_to_all x1, waiting for transfers between devices, one_device(): everything = lax.all_to_all(merged, ('y', *X), 0, 0, tiled=True)  7.44 us
    all_to_all x1, starting transfers between devices, one_device(): everything = lax.all_to_all(merged, ('y', *X), 0, 0, tiled=True)  4.41 us
  transfers between devices with their start and end apart: 14, of which 6 were waited for; matrix products, arithmetic and copies ran while one was open for 1% of the time, Pallas kernels for 4%

commit v1 on v0

--- a/solution.py
+++ b/solution.py
@@ -100,32 +100,25 @@
         out_ref[at, 2 * nx * per * half :] = in_ref[z, 0, 2 * per * half :]
 
 
-def logits_kernel(base_ref, where_ref, *refs):
-    toks, heads = refs[:8], refs[8:16]
-    out_ref, lhs, held, even, odd, sem = refs[16:]
-    copies = [pltpu.make_async_copy(heads[i], held.at[i], sem.at[i]) for i in range(8)]
-    for copy in copies:
-        copy.start()
+def place_lines(tok, lhs, line):
     half = 16
-    share, lines, _ = toks[0].shape
+    share, lines, _ = tok.shape
     per = (lines - 8) // half // 2
-    nz = 2 * share
-    ny = len(toks) // 2
-    total = ny * nz * half
-    columns = held.shape[2]
+    for at in range(share):
+        for m in range(2):
+            for k in range(per):
+                t = m * per + k
+                lhs[m, line : line + half, k * LANES : (k + 1) * LANES] = tok[
+                    at, t * half : (t + 1) * half
+                ]
+        line += half
+
+
+def columns_of(digit_refs):
     target, place = [], []
-    for y in range(ny):
-        for z in range(nz):
-            tok = toks[2 * y + z // share]
-            at = z % share
-            line = (y * nz + z) * half
-            for m in range(2):
-                for k in range(per):
-                    t = m * per + k
-                    lhs[m, line : line + half, k * LANES : (k + 1) * LANES] = tok[
-                        at, t * half : (t + 1) * half
-                    ]
-            digit = tok[at, 2 * per * half :].astype(f32)
+    for ref in digit_refs:
+        for at in range(ref.shape[0]):
+            digit = ref[at].astype(f32)
             for g in (0, 4):
                 target.append(
                     digit[:, g : g + 1]
@@ -133,66 +126,130 @@
                     + 4096.0 * digit[:, g + 2 : g + 3]
                 )
                 place.append(digit[:, g + 3 : g + 4])
-    target = jnp.concatenate(target, axis=0).astype(jnp.int32)
-    place = jnp.concatenate(place, axis=0)
+    return jnp.concatenate(target, axis=0).astype(jnp.int32), jnp.concatenate(place, axis=0)
+
+
+def scores(lhs, rows, target, shards, heads, base_ref, buffers, waits):
+    total, columns = rows.stop - rows.start, heads.shape[2]
     column = iota((total, columns), 1)
 
     def product(i, out):
-        for k in range(8):
-
-            @pl.when(i == k)
-            def _():
-                copies[k].wait()
-
-        out[...] = jnp.dot(lhs[i // 4], held[i], preferred_element_type=f32)
+        if i in waits:
+            waits.pop(i).wait()
+        out[0:total] = jnp.dot(lhs[i // 4, rows], heads[i], preferred_element_type=f32)
 
     def reduce(i, out, state):
+        values = out[0:total]
+        new_high = jnp.max(values, axis=1, keepdims=True)
+        match = column == target - base_ref[i]
+        new_hit = jnp.sum(jnp.where(match, values, 0.0), axis=1, keepdims=True)
+        if state is None:
+            part = jnp.sum(jnp.exp(values - new_high), axis=1, keepdims=True)
+            return new_high, part, new_hit
         high, summed, hit = state
-        values = out[...]
-        fresh = lax.rem(i, 4) == 0
-        here = jnp.max(values, axis=1, keepdims=True)
-        old_high = jnp.where(fresh, here, high)
-        new_high = jnp.maximum(old_high, here)
+        new_high = jnp.maximum(high, new_high)
         part = jnp.sum(jnp.exp(values - new_high), axis=1, keepdims=True)
-        summed = jnp.where(fresh, 0.0, summed) * jnp.exp(old_high - new_high) + part
-        match = column == target - base_ref[i]
-        hit = jnp.where(fresh, 0.0, hit) + jnp.sum(
-            jnp.where(match, values, 0.0), axis=1, keepdims=True
-        )
-        return new_high, summed, hit
-
-    def two(j, state):
-        product(2 * j + 1, odd)
-        state = reduce(2 * j, even, state)
-        product(2 * j + 2, even)
-        return reduce(2 * j + 1, odd, state)
-
-    zero = jnp.zeros((total, 1), f32)
-    product(0, even)
-    policy = lax.fori_loop(0, 2, two, (zero, zero, zero))
-    other = two(2, policy)
-    product(7, odd)
-    other = reduce(7, odd, reduce(6, even, other))
-    row = nz * half
-    diagonal = iota((row, LANES), 0) == iota((row, LANES), 1)
-    for y in range(ny):
-        to = where_ref[y]
-        at = slice(y * row, (y + 1) * row)
-        for v, value in enumerate(
-            (
-                policy[0] + jnp.log(policy[1]),
-                policy[2],
-                other[0] + jnp.log(other[1]),
-                other[2],
-                place,
-            )
-        ):
-            line = jnp.sum(jnp.where(diagonal, value[at], 0.0), axis=0, keepdims=True)
+        return new_high, summed * jnp.exp(high - new_high) + part, hit + new_hit
+
+    found = [None, None]
+    product(shards[0], buffers[0])
+    for n, i in enumerate(shards):
+        if n + 1 < len(shards):
+            product(shards[n + 1], buffers[(n + 1) % 2])
+        found[i // 4] = reduce(i, buffers[n % 2], found[i // 4])
+    return [
+        value for high, summed, hit in found for value in (high + jnp.log(summed), hit)
+    ]
+
+
+def as_line(column):
+    diagonal = iota((LANES, LANES), 0) == iota((LANES, LANES), 1)
+    return jnp.sum(jnp.where(diagonal, column, 0.0), axis=0, keepdims=True)
+
+
+def bring(sources, into, sem):
+    copies = [pltpu.make_async_copy(ref, into.at[k], sem.at[k]) for k, ref in enumerate(sources)]
+    for copy in copies:
+        copy.start()
+    return copies
+
+
+def local_kernel(blocks, base_ref, *refs):
+    sources, head_sources = refs[: 2 * blocks], refs[2 * blocks : 2 * blocks + 4]
+    out_ref, lhs, toks, even, odd, heads, tok_sem, sem = refs[2 * blocks + 4 :]
+    shards = (0, 1, 4, 5)
+    arriving = bring(sources, toks, tok_sem)
+    waits = {
+        i: pltpu.make_async_copy(source, heads.at[i], sem.at[n])
+        for n, (i, source) in enumerate(zip(shards, head_sources))
+    }
+    for copy in waits.values():
+        copy.start()
+    for k, copy in enumerate(arriving):
+        copy.wait()
+        place_lines(toks.at[k], lhs, k * LANES // 2)
+    last = toks.shape[2] - 8
+    target, _ = columns_of([toks.at[k, :, last:] for k in range(2 * blocks)])
+    rows = slice(0, blocks * LANES)
+    values = scores(lhs, rows, target, shards, heads, base_ref, (even, odd), waits)
+    for b in range(blocks):
+        for v, value in enumerate(values):
+            out_ref[b, v : v + 1] = as_line(value[b * LANES : (b + 1) * LANES])
+        out_ref[b, 4:8] = jnp.zeros((4, LANES), f32)
+
+
+def far_kernel(base_ref, where_ref, *refs):
+    sources, head_sources, done, packed = refs[:8], refs[8:16], refs[16:18], refs[18:20]
+    out_ref, toks, digits, lhs, even, odd, heads, tok_sem, digit_sem, pack_sem, sem = refs[20:]
+    lines = sources[0].shape[1]
+    arriving = bring(sources[6:], toks, tok_sem)
+    arriving += bring([ref.at[:, lines - 8 :] for ref in sources], digits, digit_sem)
+    for k, (start, stop) in enumerate(((0, LANES), (LANES, 3 * LANES))):
+        copy = pltpu.make_async_copy(packed[k], lhs.at[:, start:stop], pack_sem.at[k])
+        copy.start()
+        arriving.append(copy)
+    order = (2, 3, 6, 7, 0, 1, 4, 5)
+    waits = {i: pltpu.make_async_copy(head_sources[i], heads.at[i], sem.at[i]) for i in order}
+    for copy in waits.values():
+        copy.start()
+    for copy in arriving:
+        copy.wait()
+    near = 3 * LANES
+    place_lines(toks.at[0], lhs, near)
+    place_lines(toks.at[1], lhs, near + LANES // 2)
+    target, place = columns_of([digits.at[k] for k in range(8)])
+    first = scores(
+        lhs, slice(0, near), target[:near], (2, 3, 6, 7), heads, base_ref, (even, odd), waits
+    )
+    last = scores(
+        lhs,
+        slice(near, near + LANES),
+        target[near:],
+        (2, 3, 0, 1, 6, 7, 4, 5),
+        heads,
+        base_ref,
+        (even, odd),
+        waits,
+    )
+    index_z = iota((1, LANES), 1) // 16
+    for b in range(4):
+        at = slice(b * LANES, (b + 1) * LANES)
+        for v in range(5):
             if v == 4:
-                z = iota((1, LANES), 1) // half
-                line = jnp.where(line > 0.0, line + (where_ref[4 + y] + 128 * z).astype(f32), 0.0)
-            out_ref[pl.ds(4 * v + to, 1)] = line
-    out_ref[20:24] = jnp.zeros((4, LANES), f32)
+                line = as_line(place[at])
+                line = jnp.where(
+                    line > 0.0, line + (where_ref[4 + b] + 128 * index_z).astype(f32), 0.0
+                )
+            elif b == 3:
+                line = as_line(last[v])
+            else:
+                local = done[0][0, v : v + 1] if b == 0 else done[1][b - 1, v : v + 1]
+                line = as_line(first[v][at])
+                line = lse_of([line, local]) if v % 2 == 0 else line + local
+            for k in range(out_ref.shape[0]):
+                out_ref[k, pl.ds(4 * v + where_ref[b], 1)] = line
+    for k in range(out_ref.shape[0]):
+        out_ref[k, 20:24] = jnp.zeros((4, LANES), f32)
 
 
 def total_of(lines):
@@ -284,6 +341,9 @@
     doc_ref[:, 1:2] = jnp.sum(second * advantage, axis=0, keepdims=True)
 
 
+RESULT = pltpu.VMEM
+
+
 def shape_of(shape, dtype):
     return jax.ShapeDtypeStruct(shape, dtype)
 
@@ -318,13 +378,14 @@
     near_policy = lax.ppermute(head_policy, X, pair_policy)
     near_reference = lax.ppermute(head_reference, X, pair_reference)
     swapped = [shifted(near_policy, "c", 1), shifted(near_reference, "c", 1)]
+    other = [shifted(head_policy, "c", 1), shifted(head_reference, "c", 1)]
     heads = [
         head_policy,
-        shifted(head_policy, "c", 1),
+        other[0],
         near_policy,
         swapped[0],
         head_reference,
-        shifted(head_reference, "c", 1),
+        other[1],
         near_reference,
         swapped[1],
     ]
@@ -359,10 +420,11 @@
         out_specs=[VMEM] * 2,
         name="norm",
     )(got, gain_policy[None, :], gain_reference[None, :])
-    below = [shifted(part, "y", 1) for part in own]
-    above = [shifted(part, "y", -1) for part in own]
+    below_first, above_first = shifted(own[0], "y", 1), shifted(own[1], "y", -1)
+    below_second, above_second = shifted(own[1], "y", 1), shifted(own[0], "y", -1)
+    below, above = (below_first, below_second), (above_second, above_first)
     far = [shifted(below[0], "y", 1), shifted(above[1], "y", -1)]
-    lengths, _ = lax.optimization_barrier((doc_lengths, (below, above)))
+    lengths, _ = lax.optimization_barrier((doc_lengths, (below_first, above_first)))
     table = pl.pallas_call(
         tables_kernel,
         out_shape=shape_of((LANES, LANES), f32),
@@ -378,33 +440,61 @@
     y = lax.axis_index("y")
     order = [y, (y + ny - 1) % ny, (y + 1) % ny, (y + 2) % ny]
     where = jnp.stack(order + [(row * nz * 2 + c) * tok for row in order]).astype(jnp.int32)
+    group = 2 * nz
+
+    params = pltpu.CompilerParams(vmem_limit_bytes=24 * 1024 * 1024)
+    depth, chunk = nx * width, own[0].shape
+    cost = functools.partial(pl.CostEstimate, bytes_accessed=1 << 24, transcendentals=0)
+
+    def local(tokens):
+        blocks = len(tokens) // 2
+        total = blocks * nz * half
+        return pl.pallas_call(
+            functools.partial(local_kernel, blocks),
+            out_shape=(shape_of((blocks, 8, LANES), f32), shape_of((2, total, depth), bf16)),
+            in_specs=[SMEM] + [ANY] * (len(tokens) + 4),
+            out_specs=(VMEM, VMEM),
+            scratch_shapes=[
+                pltpu.VMEM((len(tokens), *chunk), bf16),
+                pltpu.VMEM((total, columns), f32),
+                pltpu.VMEM((total, columns), f32),
+                pltpu.VMEM((8, depth, columns), bf16),
+                pltpu.SemaphoreType.DMA((len(tokens),)),
+                pltpu.SemaphoreType.DMA((4,)),
+            ],
+            compiler_params=params,
+            cost_estimate=cost(flops=8 * total * depth * columns),
+        )(bases, *tokens, heads[0], heads[1], heads[4], heads[5])
+
+    mine, mine_lhs = local(own)
+    beside, beside_lhs = local((*below, *above))
     total = ny * nz * half
     stats = pl.pallas_call(
-        logits_kernel,
-        out_shape=shape_of((24, LANES), f32),
-        in_specs=[SMEM] * 2 + [VMEM] * 8 + [ANY] * 8,
+        far_kernel,
+        out_shape=RESULT((group, 24, LANES), f32),
+        in_specs=[SMEM] * 2 + [ANY] * 16 + [VMEM] * 2 + [ANY] * 2,
         out_specs=VMEM,
         scratch_shapes=[
-            pltpu.VMEM((2, total, nx * width), bf16),
-            pltpu.VMEM((8, nx * width, columns), bf16),
-            pltpu.VMEM((total, columns), f32),
-            pltpu.VMEM((total, columns), f32),
+            pltpu.VMEM((2, *chunk), bf16),
+            pltpu.VMEM((8, chunk[0], 8, LANES), bf16),
+            pltpu.VMEM((2, total, depth), bf16),
+            pltpu.VMEM((total - LANES, columns), f32),
+            pltpu.VMEM((total - LANES, columns), f32),
+            pltpu.VMEM((8, depth, columns), bf16),
+            pltpu.SemaphoreType.DMA((2,)),
+            pltpu.SemaphoreType.DMA((8,)),
+            pltpu.SemaphoreType.DMA((2,)),
             pltpu.SemaphoreType.DMA((8,)),
         ],
-        compiler_params=pltpu.CompilerParams(vmem_limit_bytes=48 * 1024 * 1024),
-        cost_estimate=pl.CostEstimate(
-            flops=2 * 8 * total * nx * width * columns, bytes_accessed=1 << 24, transcendentals=0
-        ),
-        name="logits",
-    )(bases, where, *own, *below, *above, *far, *heads)
-    group = 2 * nz
-    gathered = lax.all_to_all(
-        jnp.broadcast_to(stats[None], (group, *stats.shape)), ("z", "c"), 0, 0, tiled=True
-    )
+        compiler_params=params,
+        cost_estimate=cost(flops=10 * total * depth * columns),
+        name="logits_far",
+    )(bases, where, *own, *below, *above, *far, *heads, mine, beside, mine_lhs, beside_lhs)
+    gathered = lax.all_to_all(stats, ("z", "c"), 0, 0, tiled=True)
     group = ny * nx
     merged = pl.pallas_call(
         merge_kernel,
-        out_shape=shape_of((group, 5, 8, LANES), f32),
+        out_shape=RESULT((group, 5, 8, LANES), f32),
         in_specs=[VMEM],
         out_specs=VMEM,
         name="merge",

time: 137 us -> 134 us (0.978)
  waiting for transfers between devices: 60.6 us -> 52 us
  Pallas kernels: 20.6 us -> 27.4 us
    ppermute x10, waiting for transfers between devices: 25.3 us -> 16.7 us  [shifted(): return lax.ppermute(x, axis, [(i, (i + by) % n) for i in range(n)])]
    pallas_call x2 -> x4, Pallas kernels: 12.4 us -> 19.2 us  [the longest x2 9.01 us: local(): pl.pallas_call(functools.partial(local_kernel, blocks), out_shape=(shape_...]
    unnamed x14 -> x20, local copies, waits for them, and re-layouts: 3.64 us -> 3.49 us
  transfers between devices with their start and end apart: 14 -> 14, of which waited for: 6 -> 4; matrix products, arithmetic and copies ran while one was open for 1% -> 1% of each run, Pallas kernels for 4% -> 11%
where the time goes in v1:
time: 134 us
  waiting for transfers between devices  52 us (39%)
  starting transfers between devices  28.8 us (21%)
  Pallas kernels  27.4 us (20%)
  blocking collectives  20.1 us (15%)
  local copies, waits for them, and re-layouts  4.85 us (4%)
    ppermute x1, waiting for transfers between devices, one_device(): near_reference = lax.ppermute(head_reference, X, pair_reference)  27.6 us
    all_to_all x1, blocking collectives, one_device(): gathered = lax.all_to_all(stats, ('z', 'c'), 0, 0, tiled=True)  20.1 us
    ppermute x10, waiting for transfers between devices, shifted(): return lax.ppermute(x, axis, [(i, (i + by) % n) for i in range(n)])  16.7 us
    ppermute x10, starting transfers between devices, shifted(): return lax.ppermute(x, axis, [(i, (i + by) % n) for i in range(n)])  11.8 us
    all_to_all x1, starting transfers between devices, one_device(): lax.all_to_all(sent.reshape(nz * nx, lines, LANES), ('z', *X), 0, 0, tile...  10 us
    pallas_call x2, Pallas kernels, local(): pl.pallas_call(functools.partial(local_kernel, blocks), out_shape=(shape_...  9.01 us
    pallas_call x1, Pallas kernels, one_device(): pl.pallas_call(far_kernel, out_shape=RESULT((group, 24, LANES), f32), in_...  8.47 us
    all_to_all x1, waiting for transfers between devices, one_device(): everything = lax.all_to_all(merged, ('y', *X), 0, 0, tiled=True)  7.69 us
  transfers between devices with their start and end apart: 14, of which 4 were waited for; matrix products, arithmetic and copies ran while one was open for 1% of the time, Pallas kernels for 11%

profile of v1, /device:TPU:1, one launch (start us, length us, event | category | flops | bytes accessed | tf_op | source)
XLA Modules:
  0.0 133.8 jit_solution(14374960253542106642)
XLA Ops:
  0.6 0.0 copy-start
  0.6 0.0 copy-start.8
  0.7 0.0 copy-start.9
  0.7 3.4 %collective-permute-start.10 = (bf16[1536,512]{1,0:T(8,128)(2,1)}, bf16[1536,512]{1,0:T(8,128)(2,1)}, u32[]{:S(2)}, u32[]{:S(2)}) collective-permute-start(bf16[1536,512]{1,0:T(8,128)(2,1)} %refs_12_.1), channel_id=1, source_target_pairs={{0,3},{1,2},{2,1},{3,0},{4,7},{5,6},{6,5},{7,4},{8,11},{9,10},{10,... | collective-permute-start | bytes 4718600 | tf_op jit(solution)/shard_map/ppermute | solution.py:379
  4.0 0.0 collective-permute-start.7
  4.0 2.0 %pick.1 = bf16[8,4,104,128]{3,2,1,0:T(8,128)(2,1)} custom-call(bf16[64,384]{1,0:T(8,128)(2,1)} %hp_ref.1, bf16[64,384]{1,0:T(8,128)(2,1)} %hr_ref.1, s32[1,64]{1,0:T(1,128)} %bitcast.25, s32[1,64]{1,0:T(1,128)} %bitcast.26), custom_call_target="tpu_custom_call" | custom-call | tf_op jit(solution)/shard_map/pick/pallas_call | solution.py:405
  6.1 0.0 copy-start.1
  6.1 10.0 %all-to-all-start = ((bf16[32,104,128]{2,1,0:T(8,128)(2,1)}), bf16[32,104,128]{2,1,0:T(8,128)(2,1)}, u32[]{:S(2)}, u32[]{:S(2)}) async-start(bf16[32,104,128]{2,1,0:T(8,128)(2,1)} %bitcast.24), calls=%async_computation | async-start | bytes 1703936 | tf_op jit(solution)/shard_map/all_to_all | solution.py:412
  16.1 0.0 copy-done
  16.1 1.6 %collective-permute-start.6 = (bf16[1536,512]{1,0:T(8,128)(2,1)S(1)}, bf16[1536,512]{1,0:T(8,128)(2,1)}, u32[]{:S(2)}, u32[]{:S(2)}) collective-permute-start(bf16[1536,512]{1,0:T(8,128)(2,1)S(1)} %copy-done), channel_id=1, source_target_pairs={{0,4},{4,0},{1,5},{5,1},{2,6},{6,2},{3,7},{7,3},{8,12},{12,8},{9,1... | collective-permute-start | bytes 4718600 | tf_op jit(solution)/shard_map/ppermute | solution.py:353
  17.7 0.1 collective-permute-start.9
  17.8 27.6 %collective-permute-done.10.refs_14_ = bf16[1536,512]{1,0:T(8,128)(2,1)} collective-permute-done((bf16[1536,512]{1,0:T(8,128)(2,1)}, bf16[1536,512]{1,0:T(8,128)(2,1)}, u32[]{:S(2)}, u32[]{:S(2)}) %collective-permute-start.10) | collective-permute-done | bytes 1572896 | tf_op jit(solution)/shard_map/ppermute | solution.py:379
  45.4 2.8 %collective-permute-start.11 = (bf16[1536,512]{1,0:T(8,128)(2,1)}, bf16[1536,512]{1,0:T(8,128)(2,1)}, u32[]{:S(2)}, u32[]{:S(2)}) collective-permute-start(bf16[1536,512]{1,0:T(8,128)(2,1)} %collective-permute-done.10.refs_14_), channel_id=1, source_target_pairs={{0,4},{4,0},{1,5},{5,1},{2,6},{6,2},{3,7},{7,3},{8,12},{12,8},{9,1... | collective-permute-start | bytes 4718600 | tf_op jit(solution)/shard_map/ppermute | solution.py:353
  48.3 0.0 collective-permute-done.7.refs_10_
  48.3 1.5 %collective-permute-start.8 = (bf16[1536,512]{1,0:T(8,128)(2,1)}, bf16[1536,512]{1,0:T(8,128)(2,1)}, u32[]{:S(2)}, u32[]{:S(2)}) collective-permute-start(bf16[1536,512]{1,0:T(8,128)(2,1)} %collective-permute-done.7.refs_10_), channel_id=1, source_target_pairs={{0,4},{4,0},{1,5},{5,1},{2,6},{6,2},{3,7},{7,3},{8,12},{12,8},{9,1... | collective-permute-start | bytes 4718600 | tf_op jit(solution)/shard_map/ppermute | solution.py:353
  49.7 0.0 copy-done.8
  49.7 0.6 broadcast_in_dim.23.gp_ref
  50.3 0.0 copy-done.9
  50.3 0.6 broadcast_in_dim.24.gr_ref
  50.9 0.0 all-to-all-done
  50.9 2.3 %norm.1 = (bf16[4,392,128]{2,1,0:T(8,128)(2,1)}, bf16[4,392,128]{2,1,0:T(8,128)(2,1)}) custom-call(bf16[8,4,104,128]{3,2,1,0:T(8,128)(2,1)} %bitcast.17.in_ref, bf16[1,1536]{1,0:T(2,128)(2,1)} %broadcast_in_dim.23.gp_ref, bf16[1,1536]{1,0:T(2,128)(2,1)} %broadcast_in_dim.24.gr_ref), custom_call_target="tpu_custom_call" | custom-call | tf_op jit(solution)/shard_map/norm/pallas_call | solution.py:416
  53.3 1.3 collective-permute-start
  54.6 0.0 collective-permute-done.6.refs_3_.refs_5_.refs_9_
  54.6 1.5 %collective-permute-start.3 = (bf16[4,392,128]{2,1,0:T(8,128)(2,1)}, bf16[4,392,128]{2,1,0:T(8,128)(2,1)}, u32[]{:S(2)}, u32[]{:S(2)}) collective-permute-start(bf16[4,392,128]{2,1,0:T(8,128)(2,1)} %get-tuple-element.12.refs_1_), channel_id=1, source_target_pairs={{0,192},{64,0},{128,64},{192,128},{1,193},{65,1},{129,65},{193,129... | collective-permute-start | bytes 1204232 | tf_op jit(solution)/shard_map/ppermute | solution.py:353
  56.1 0.0 collective-permute-done.9.refs_5_.refs_7_.refs_13_
  56.1 0.0 collective-permute-start.1
  56.1 9.6 %collective-permute-done.refs_0_.refs_2_ = bf16[4,392,128]{2,1,0:T(8,128)(2,1)S(1)} collective-permute-done((bf16[4,392,128]{2,1,0:T(8,128)(2,1)}, bf16[4,392,128]{2,1,0:T(8,128)(2,1)S(1)}, u32[]{:S(2)}, u32[]{:S(2)}) %collective-permute-start) | collective-permute-done | bytes 401440 | tf_op jit(solution)/shard_map/ppermute | solution.py:353
  65.7 1.5 %collective-permute-start.2 = (bf16[4,392,128]{2,1,0:T(8,128)(2,1)}, bf16[4,392,128]{2,1,0:T(8,128)(2,1)}, u32[]{:S(2)}, u32[]{:S(2)}) collective-permute-start(bf16[4,392,128]{2,1,0:T(8,128)(2,1)} %get-tuple-element.11.refs_0_), channel_id=1, source_target_pairs={{0,192},{64,0},{128,64},{192,128},{1,193},{65,1},{129,65},{193,129... | collective-permute-start | bytes 1204232 | tf_op jit(solution)/shard_map/ppermute | solution.py:353
  67.2 0.0 collective-permute-done.3.refs_3_.refs_5_
  67.2 0.0 collective-permute-start.4
  67.2 7.1 %collective-permute-done.1.refs_1_.refs_3_ = bf16[4,392,128]{2,1,0:T(8,128)(2,1)S(1)} collective-permute-done((bf16[4,392,128]{2,1,0:T(8,128)(2,1)}, bf16[4,392,128]{2,1,0:T(8,128)(2,1)S(1)}, u32[]{:S(2)}, u32[]{:S(2)}) %collective-permute-start.1) | collective-permute-done | bytes 401440 | tf_op jit(solution)/shard_map/ppermute | solution.py:353
  74.3 0.0 copy-start.5
  74.3 0.7 copy-done.5
  75.0 1.5 %collective-permute-start.5 = (bf16[4,392,128]{2,1,0:T(8,128)(2,1)}, bf16[4,392,128]{2,1,0:T(8,128)(2,1)}, u32[]{:S(2)}, u32[]{:S(2)}) collective-permute-start(bf16[4,392,128]{2,1,0:T(8,128)(2,1)} %collective-permute-done.3.refs_3_.refs_5_), channel_id=1, source_target_pairs={{0,192},{64,0},{128,64},{192,128},{1,193},{65,1},{129,65},{193,129... | collective-permute-start | bytes 1204232 | tf_op jit(solution)/shard_map/ppermute | solution.py:353
  76.5 0.1 stack.59.base_ref
  76.6 0.1 stack.68.where_ref
  76.7 0.0 copy-done.1
  76.7 0.0 copy-start.2
  76.7 1.0 copy-done.2
  77.7 0.0 copy-start.4
  77.7 1.0 copy-done.4
  78.7 0.0 copy-start.6
  78.7 3.9 %shard_map.122 = (f32[1,8,128]{2,1,0:T(8,128)S(1)}, bf16[2,128,1536]{2,1,0:T(8,128)(2,1)S(1)}) custom-call(s32[8]{0:T(128)S(1)} %stack.59.base_ref, bf16[4,392,128]{2,1,0:T(8,128)(2,1)S(1)} %copy-done.2, bf16[4,392,128]{2,1,0:T(8,128)(2,1)S(1)} %copy-done.4, bf16[1536,512]{1,0:T(8,128)(2,1)S(1)} %copy-done, ...), custom_call_target="tpu_custom_call" | custom-call | flops 805306368 | bytes 16777216 | tf_op jit(solution)/shard_map/pallas_call | solution.py:452
  82.6 0.0 copy-start.3
  82.6 0.0 collective-permute-done.2.refs_2_.refs_4_
  82.6 0.0 copy-done.6
  82.7 5.1 %shard_map.123 = (f32[2,8,128]{2,1,0:T(8,128)S(1)}, bf16[2,256,1536]{2,1,0:T(8,128)(2,1)S(1)}) custom-call(s32[8]{0:T(128)S(1)} %stack.59.base_ref, bf16[4,392,128]{2,1,0:T(8,128)(2,1)S(1)} %collective-permute-done.refs_0_.refs_2_, bf16[4,392,128]{2,1,0:T(8,128)(2,1)S(1)} %copy-done.6, bf16[4,392,128]{2,1,0:T(8,128)(2,1)} %collective-permute-done.2.refs_2_.refs_4_, ...), custom_call_target="tpu_custom_call" | custom-call | flops 1610612736 | bytes 16777216 | tf_op jit(solution)/shard_map/pallas_call | solution.py:452
  87.7 0.0 collective-permute-done.4.refs_6_
  87.8 0.0 collective-permute-done.5.refs_7_
  87.8 0.0 collective-permute-done.11.refs_15_
  87.8 0.0 collective-permute-done.8.refs_11_
  87.8 0.0 copy-done.3
  87.8 8.5 %logits_far.1 = f32[16,24,128]{2,1,0:T(8,128)S(1)} custom-call(s32[8]{0:T(128)S(1)} %stack.59.base_ref, s32[8]{0:T(128)S(1)} %stack.68.where_ref, bf16[4,392,128]{2,1,0:T(8,128)(2,1)S(1)} %copy-done.3, bf16[4,392,128]{2,1,0:T(8,128)(2,1)S(1)} %copy-done.4, bf16[4,392,128]{2,1,0:T(8,128)(2,1)S(1)} %collective-permute-done.refs_0_.refs_2_, ...), custom_call_target="tpu_custom_call" | custom-call | flops 4026531840 | bytes 16777216 | tf_op jit(solution)/shard_map/logits_far/pallas_call | solution.py:472
  96.3 20.1 %all_to_all.15.in_ref = f32[16,24,128]{2,1,0:T(8,128)} all-to-all(f32[16,24,128]{2,1,0:T(8,128)S(1)} %logits_far.1), channel_id=1, replica_groups=mesh['y'=4,'z'=8,'c'=2,'xh'=2,'xl'=2] {'z','c'}, dimensions={0} | all-to-all | bytes 393216 | tf_op jit(solution)/shard_map/all_to_all | solution.py:493
  116.3 1.7 %merge.1 = f32[16,5,8,128]{3,2,1,0:T(8,128)} custom-call(f32[16,24,128]{2,1,0:T(8,128)} %all_to_all.15.in_ref), custom_call_target="tpu_custom_call" | custom-call | tf_op jit(solution)/shard_map/merge/pallas_call | solution.py:495
  118.0 3.5 %all-to-all-start.2 = ((f32[16,5,8,128]{3,2,1,0:T(8,128)}), f32[16,5,8,128]{3,2,1,0:T(8,128)S(1)}, u32[]{:S(2)}, u32[]{:S(2)}) async-start(f32[16,5,8,128]{3,2,1,0:T(8,128)} %merge.1), calls=%async_computation.2 | async-start | bytes 655360 | tf_op jit(solution)/shard_map/all_to_all | solution.py:502
  121.6 1.7 %tables.1.table_ref = f32[128,128]{1,0:T(8,128)} custom-call(s32[1]{0:T(128)} %bitcast.18.me_ref, s32[1,128]{1,0:T(1,128)} %bitcast.27, s32[1,128]{1,0:T(1,128)} %bitcast.28, f32[1,128]{1,0:T(1,128)} %bitcast.29), custom_call_target="tpu_custom_call" | custom-call | tf_op jit(solution)/shard_map/tables/pallas_call | solution.py:428
  123.3 7.7 %all-to-all-done.2.in_ref = f32[16,5,8,128]{3,2,1,0:T(8,128)S(1)} async-done(((f32[16,5,8,128]{3,2,1,0:T(8,128)}), f32[16,5,8,128]{3,2,1,0:T(8,128)S(1)}, u32[]{:S(2)}, u32[]{:S(2)}) %all-to-all-start.2) | async-done | bytes 327712 | tf_op jit(solution)/shard_map/all_to_all | solution.py:502
  131.0 0.0 copy-start.7
  131.0 0.7 copy-done.7
  131.7 2.1 %docs.1 = (f32[1,128]{1,0:T(1,128)}, f32[1,2]{1,0:T(1,128)}) custom-call(f32[16,5,8,128]{3,2,1,0:T(8,128)} %copy-done.7, f32[128,128]{1,0:T(8,128)} %tables.1.table_ref), custom_call_target="tpu_custom_call" | custom-call | tf_op jit(solution)/shard_map/docs/pallas_call | solution.py:503
Async XLA Ops:
  0.6 15.5 %copy-start = (bf16[1536,512]{1,0:T(8,128)(2,1)S(1)}, bf16[1536,512]{1,0:T(8,128)(2,1)}, u32[]{:S(2)}) copy-start(bf16[1536,512]{1,0:T(8,128)(2,1)} %refs_8_.1) | copy-start | bytes 4718596
  0.6 49.1 %copy-start.8 = (bf16[1536]{0:T(1024)(128)(2,1)S(1)}, bf16[1536]{0:T(1024)(128)(2,1)}, u32[]{:S(2)}) copy-start(bf16[1536]{0:T(1024)(128)(2,1)} %param.13) | copy-start | bytes 9220
  0.7 49.7 %copy-start.9 = (bf16[1536]{0:T(1024)(128)(2,1)S(1)}, bf16[1536]{0:T(1024)(128)(2,1)}, u32[]{:S(2)}) copy-start(bf16[1536]{0:T(1024)(128)(2,1)} %param.14) | copy-start | bytes 9220
  0.7 44.8 %collective-permute-start.10 = (bf16[1536,512]{1,0:T(8,128)(2,1)}, bf16[1536,512]{1,0:T(8,128)(2,1)}, u32[]{:S(2)}, u32[]{:S(2)}) collective-permute-start(bf16[1536,512]{1,0:T(8,128)(2,1)} %refs_12_.1), channel_id=1, source_target_pairs={{0,3},{1,2},{2,1},{3,0},{4,7},{5,6},{6,5},{7,4},{8,11},{9,10},{10,... | collective-permute-start | bytes 4718600 | tf_op jit(solution)/shard_map/ppermute | solution.py:379
  4.0 44.2 %collective-permute-start.7 = (bf16[1536,512]{1,0:T(8,128)(2,1)}, bf16[1536,512]{1,0:T(8,128)(2,1)}, u32[]{:S(2)}, u32[]{:S(2)}) collective-permute-start(bf16[1536,512]{1,0:T(8,128)(2,1)} %refs_8_.1), channel_id=1, source_target_pairs={{0,1},{1,0},{2,3},{3,2},{4,5},{5,4},{6,7},{7,6},{8,9},{9,8},{10,11... | collective-permute-start | bytes 4718600 | tf_op jit(solution)/shard_map/ppermute | solution.py:378
  6.1 70.6 %copy-start.1 = (bf16[1536,512]{1,0:T(8,128)(2,1)S(1)}, bf16[1536,512]{1,0:T(8,128)(2,1)}, u32[]{:S(2)}) copy-start(bf16[1536,512]{1,0:T(8,128)(2,1)} %refs_12_.1) | copy-start | bytes 4718596
  6.1 44.9 %all-to-all-start = ((bf16[32,104,128]{2,1,0:T(8,128)(2,1)}), bf16[32,104,128]{2,1,0:T(8,128)(2,1)}, u32[]{:S(2)}, u32[]{:S(2)}) async-start(bf16[32,104,128]{2,1,0:T(8,128)(2,1)} %bitcast.24), calls=%async_computation | async-start | bytes 1703936 | tf_op jit(solution)/shard_map/all_to_all | solution.py:412
  16.1 38.5 %collective-permute-start.6 = (bf16[1536,512]{1,0:T(8,128)(2,1)S(1)}, bf16[1536,512]{1,0:T(8,128)(2,1)}, u32[]{:S(2)}, u32[]{:S(2)}) collective-permute-start(bf16[1536,512]{1,0:T(8,128)(2,1)S(1)} %copy-done), channel_id=1, source_target_pairs={{0,4},{4,0},{1,5},{5,1},{2,6},{6,2},{3,7},{7,3},{8,12},{12,8},{9,1... | collective-permute-start | bytes 4718600 | tf_op jit(solution)/shard_map/ppermute | solution.py:353
  17.7 38.4 %collective-permute-start.9 = (bf16[1536,512]{1,0:T(8,128)(2,1)}, bf16[1536,512]{1,0:T(8,128)(2,1)}, u32[]{:S(2)}, u32[]{:S(2)}) collective-permute-start(bf16[1536,512]{1,0:T(8,128)(2,1)} %refs_12_.1), channel_id=1, source_target_pairs={{0,4},{4,0},{1,5},{5,1},{2,6},{6,2},{3,7},{7,3},{8,12},{12,8},{9,1... | collective-permute-start | bytes 4718600 | tf_op jit(solution)/shard_map/ppermute | solution.py:353
  45.4 42.3 %collective-permute-start.11 = (bf16[1536,512]{1,0:T(8,128)(2,1)}, bf16[1536,512]{1,0:T(8,128)(2,1)}, u32[]{:S(2)}, u32[]{:S(2)}) collective-permute-start(bf16[1536,512]{1,0:T(8,128)(2,1)} %collective-permute-done.10.refs_14_), channel_id=1, source_target_pairs={{0,4},{4,0},{1,5},{5,1},{2,6},{6,2},{3,7},{7,3},{8,12},{12,8},{9,1... | collective-permute-start | bytes 4718600 | tf_op jit(solution)/shard_map/ppermute | solution.py:353
  48.3 39.5 %collective-permute-start.8 = (bf16[1536,512]{1,0:T(8,128)(2,1)}, bf16[1536,512]{1,0:T(8,128)(2,1)}, u32[]{:S(2)}, u32[]{:S(2)}) collective-permute-start(bf16[1536,512]{1,0:T(8,128)(2,1)} %collective-permute-done.7.refs_10_), channel_id=1, source_target_pairs={{0,4},{4,0},{1,5},{5,1},{2,6},{6,2},{3,7},{7,3},{8,12},{12,8},{9,1... | collective-permute-start | bytes 4718600 | tf_op jit(solution)/shard_map/ppermute | solution.py:353
  53.3 12.4 %collective-permute-start = (bf16[4,392,128]{2,1,0:T(8,128)(2,1)}, bf16[4,392,128]{2,1,0:T(8,128)(2,1)S(1)}, u32[]{:S(2)}, u32[]{:S(2)}) collective-permute-start(bf16[4,392,128]{2,1,0:T(8,128)(2,1)} %get-tuple-element.11.refs_0_), channel_id=1, source_target_pairs={{0,64},{64,128},{128,192},{192,0},{1,65},{65,129},{129,193},{193,1... | collective-permute-start | bytes 1204232 | tf_op jit(solution)/shard_map/ppermute | solution.py:353
  54.6 12.6 %collective-permute-start.3 = (bf16[4,392,128]{2,1,0:T(8,128)(2,1)}, bf16[4,392,128]{2,1,0:T(8,128)(2,1)}, u32[]{:S(2)}, u32[]{:S(2)}) collective-permute-start(bf16[4,392,128]{2,1,0:T(8,128)(2,1)} %get-tuple-element.12.refs_1_), channel_id=1, source_target_pairs={{0,192},{64,0},{128,64},{192,128},{1,193},{65,1},{129,65},{193,129... | collective-permute-start | bytes 1204232 | tf_op jit(solution)/shard_map/ppermute | solution.py:353
  56.1 18.2 %collective-permute-start.1 = (bf16[4,392,128]{2,1,0:T(8,128)(2,1)}, bf16[4,392,128]{2,1,0:T(8,128)(2,1)S(1)}, u32[]{:S(2)}, u32[]{:S(2)}) collective-permute-start(bf16[4,392,128]{2,1,0:T(8,128)(2,1)} %get-tuple-element.12.refs_1_), channel_id=1, source_target_pairs={{0,64},{64,128},{128,192},{192,0},{1,65},{65,129},{129,193},{193,1... | collective-permute-start | bytes 1204232 | tf_op jit(solution)/shard_map/ppermute | solution.py:353
  65.7 17.0 %collective-permute-start.2 = (bf16[4,392,128]{2,1,0:T(8,128)(2,1)}, bf16[4,392,128]{2,1,0:T(8,128)(2,1)}, u32[]{:S(2)}, u32[]{:S(2)}) collective-permute-start(bf16[4,392,128]{2,1,0:T(8,128)(2,1)} %get-tuple-element.11.refs_0_), channel_id=1, source_target_pairs={{0,192},{64,0},{128,64},{192,128},{1,193},{65,1},{129,65},{193,129... | collective-permute-start | bytes 1204232 | tf_op jit(solution)/shard_map/ppermute | solution.py:353
  67.2 20.6 %collective-permute-start.4 = (bf16[4,392,128]{2,1,0:T(8,128)(2,1)S(1)}, bf16[4,392,128]{2,1,0:T(8,128)(2,1)}, u32[]{:S(2)}, u32[]{:S(2)}) collective-permute-start(bf16[4,392,128]{2,1,0:T(8,128)(2,1)S(1)} %collective-permute-done.refs_0_.refs_2_), channel_id=1, source_target_pairs={{0,64},{64,128},{128,192},{192,0},{1,65},{65,129},{129,193},{193,1... | collective-permute-start | bytes 1204232 | tf_op jit(solution)/shard_map/ppermute | solution.py:353
  74.3 0.8 copy-start.5
  75.0 12.8 %collective-permute-start.5 = (bf16[4,392,128]{2,1,0:T(8,128)(2,1)}, bf16[4,392,128]{2,1,0:T(8,128)(2,1)}, u32[]{:S(2)}, u32[]{:S(2)}) collective-permute-start(bf16[4,392,128]{2,1,0:T(8,128)(2,1)} %collective-permute-done.3.refs_3_.refs_5_), channel_id=1, source_target_pairs={{0,192},{64,0},{128,64},{192,128},{1,193},{65,1},{129,65},{193,129... | collective-permute-start | bytes 1204232 | tf_op jit(solution)/shard_map/ppermute | solution.py:353
  76.7 1.0 copy-start.2
  77.7 1.0 copy-start.4
  78.7 4.0 %copy-start.6 = (bf16[4,392,128]{2,1,0:T(8,128)(2,1)S(1)}, bf16[4,392,128]{2,1,0:T(8,128)(2,1)}, u32[]{:S(2)}) copy-start(bf16[4,392,128]{2,1,0:T(8,128)(2,1)} %copy-done.5) | copy-start | bytes 1204228
  82.6 5.2 %copy-start.3 = (bf16[4,392,128]{2,1,0:T(8,128)(2,1)S(1)}, bf16[4,392,128]{2,1,0:T(8,128)(2,1)}, u32[]{:S(2)}) copy-start(bf16[4,392,128]{2,1,0:T(8,128)(2,1)} %get-tuple-element.11.refs_0_) | copy-start | bytes 1204228
  118.0 12.9 %all-to-all-start.2 = ((f32[16,5,8,128]{3,2,1,0:T(8,128)}), f32[16,5,8,128]{3,2,1,0:T(8,128)S(1)}, u32[]{:S(2)}, u32[]{:S(2)}) async-start(f32[16,5,8,128]{3,2,1,0:T(8,128)} %merge.1), calls=%async_computation.2 | async-start | bytes 655360 | tf_op jit(solution)/shard_map/all_to_all | solution.py:502
  131.0 0.7 copy-start.7

commit v2 on v1

--- a/solution.py
+++ b/solution.py
@@ -198,7 +198,7 @@
         out_ref[b, 4:8] = jnp.zeros((4, LANES), f32)
 
 
-def far_kernel(base_ref, where_ref, *refs):
+def far_kernel(base_ref, *refs):
     sources, head_sources, done, packed = refs[:8], refs[8:16], refs[16:18], refs[18:20]
     out_ref, toks, digits, lhs, even, odd, heads, tok_sem, digit_sem, pack_sem, sem = refs[20:]
     lines = sources[0].shape[1]
@@ -238,7 +238,7 @@
             if v == 4:
                 line = as_line(place[at])
                 line = jnp.where(
-                    line > 0.0, line + (where_ref[4 + b] + 128 * index_z).astype(f32), 0.0
+                    line > 0.0, line + (base_ref[12 + b] + 128 * index_z).astype(f32), 0.0
                 )
             elif b == 3:
                 line = as_line(last[v])
@@ -247,7 +247,7 @@
                 line = as_line(first[v][at])
                 line = lse_of([line, local]) if v % 2 == 0 else line + local
             for k in range(out_ref.shape[0]):
-                out_ref[k, pl.ds(4 * v + where_ref[b], 1)] = line
+                out_ref[k, pl.ds(4 * v + base_ref[8 + b], 1)] = line
     for k in range(out_ref.shape[0]):
         out_ref[k, 20:24] = jnp.zeros((4, LANES), f32)
 
@@ -392,6 +392,8 @@
     x_policy = x ^ 1
     x_reference = jnp.where(x % 2 == 1, (x + 1) % nx, (x + nx - 1) % nx)
     row_of = me - c
+    y = lax.axis_index("y")
+    order = [y, (y + ny - 1) % ny, (y + 1) % ny, (y + 2) % ny]
     bases = jnp.stack(
         [
             ((row_of + core) * nx + place) * columns
@@ -399,6 +401,8 @@
             for place in (x, partner)
             for core in (c, 1 - c)
         ]
+        + order
+        + [(row * nz * 2 + c) * tok for row in order]
     ).astype(jnp.int32)
 
     lines = 2 * per * half + 8
@@ -437,9 +441,6 @@
         doc_owner[None, :],
         doc_score[None, :],
     )
-    y = lax.axis_index("y")
-    order = [y, (y + ny - 1) % ny, (y + 1) % ny, (y + 2) % ny]
-    where = jnp.stack(order + [(row * nz * 2 + c) * tok for row in order]).astype(jnp.int32)
     group = 2 * nz
 
     params = pltpu.CompilerParams(vmem_limit_bytes=24 * 1024 * 1024)
@@ -472,7 +473,7 @@
     stats = pl.pallas_call(
         far_kernel,
         out_shape=RESULT((group, 24, LANES), f32),
-        in_specs=[SMEM] * 2 + [ANY] * 16 + [VMEM] * 2 + [ANY] * 2,
+        in_specs=[SMEM] + [ANY] * 16 + [VMEM] * 2 + [ANY] * 2,
         out_specs=VMEM,
         scratch_shapes=[
             pltpu.VMEM((2, *chunk), bf16),
@@ -489,7 +490,7 @@
         compiler_params=params,
         cost_estimate=cost(flops=10 * total * depth * columns),
         name="logits_far",
-    )(bases, where, *own, *below, *above, *far, *heads, mine, beside, mine_lhs, beside_lhs)
+    )(bases, *own, *below, *above, *far, *heads, mine, beside, mine_lhs, beside_lhs)
     gathered = lax.all_to_all(stats, ("z", "c"), 0, 0, tiled=True)
     group = ny * nx
     merged = pl.pallas_call(

time: 134 us -> 134 us (level)
  no operation moved by 1% of the time
where the time goes in v2:
time: 134 us
  waiting for transfers between devices  52 us (39%)
  starting transfers between devices  28.8 us (21%)
  Pallas kernels  27.4 us (20%)
  blocking collectives  20.1 us (15%)
  local copies, waits for them, and re-layouts  4.76 us (4%)
    ppermute x1, waiting for transfers between devices, one_device(): near_reference = lax.ppermute(head_reference, X, pair_reference)  27.6 us
    all_to_all x1, blocking collectives, one_device(): gathered = lax.all_to_all(stats, ('z', 'c'), 0, 0, tiled=True)  20.1 us
    ppermute x10, waiting for transfers between devices, shifted(): return lax.ppermute(x, axis, [(i, (i + by) % n) for i in range(n)])  16.7 us
    ppermute x10, starting transfers between devices, shifted(): return lax.ppermute(x, axis, [(i, (i + by) % n) for i in range(n)])  11.8 us
    all_to_all x1, starting transfers between devices, one_device(): lax.all_to_all(sent.reshape(nz * nx, lines, LANES), ('z', *X), 0, 0, tile...  10 us
    pallas_call x2, Pallas kernels, local(): pl.pallas_call(functools.partial(local_kernel, blocks), out_shape=(shape_...  9.02 us
    pallas_call x1, Pallas kernels, one_device(): pl.pallas_call(far_kernel, out_shape=RESULT((group, 24, LANES), f32), in_...  8.48 us
    all_to_all x1, waiting for transfers between devices, one_device(): everything = lax.all_to_all(merged, ('y', *X), 0, 0, tiled=True)  7.69 us
  transfers between devices with their start and end apart: 14, of which 4 were waited for; matrix products, arithmetic and copies ran while one was open for 1% of the time, Pallas kernels for 11%

profile of v2, /device:TPU:1, one launch (start us, length us, event | category | flops | bytes accessed | tf_op | source)
XLA Modules:
  0.0 133.8 jit_solution(16179857709469197522)
XLA Ops:
  0.6 0.0 copy-start
  0.6 0.0 copy-start.8
  0.7 0.0 copy-start.9
  0.7 3.4 %collective-permute-start.10 = (bf16[1536,512]{1,0:T(8,128)(2,1)}, bf16[1536,512]{1,0:T(8,128)(2,1)}, u32[]{:S(2)}, u32[]{:S(2)}) collective-permute-start(bf16[1536,512]{1,0:T(8,128)(2,1)} %refs_12_.1), channel_id=1, source_target_pairs={{0,3},{1,2},{2,1},{3,0},{4,7},{5,6},{6,5},{7,4},{8,11},{9,10},{10,... | collective-permute-start | bytes 4718600 | tf_op jit(solution)/shard_map/ppermute | solution.py:379
  4.0 0.0 collective-permute-start.7
  4.0 2.0 %pick.1 = bf16[8,4,104,128]{3,2,1,0:T(8,128)(2,1)} custom-call(bf16[64,384]{1,0:T(8,128)(2,1)} %hp_ref.1, bf16[64,384]{1,0:T(8,128)(2,1)} %hr_ref.1, s32[1,64]{1,0:T(1,128)} %bitcast.25, s32[1,64]{1,0:T(1,128)} %bitcast.26), custom_call_target="tpu_custom_call" | custom-call | tf_op jit(solution)/shard_map/pick/pallas_call | solution.py:409
  6.1 0.0 copy-start.1
  6.1 10.0 %all-to-all-start = ((bf16[32,104,128]{2,1,0:T(8,128)(2,1)}), bf16[32,104,128]{2,1,0:T(8,128)(2,1)}, u32[]{:S(2)}, u32[]{:S(2)}) async-start(bf16[32,104,128]{2,1,0:T(8,128)(2,1)} %bitcast.24), calls=%async_computation | async-start | bytes 1703936 | tf_op jit(solution)/shard_map/all_to_all | solution.py:416
  16.1 0.0 copy-done
  16.1 1.6 %collective-permute-start.6 = (bf16[1536,512]{1,0:T(8,128)(2,1)S(1)}, bf16[1536,512]{1,0:T(8,128)(2,1)}, u32[]{:S(2)}, u32[]{:S(2)}) collective-permute-start(bf16[1536,512]{1,0:T(8,128)(2,1)S(1)} %copy-done), channel_id=1, source_target_pairs={{0,4},{4,0},{1,5},{5,1},{2,6},{6,2},{3,7},{7,3},{8,12},{12,8},{9,1... | collective-permute-start | bytes 4718600 | tf_op jit(solution)/shard_map/ppermute | solution.py:353
  17.7 0.1 collective-permute-start.9
  17.8 27.6 %collective-permute-done.10.refs_14_ = bf16[1536,512]{1,0:T(8,128)(2,1)} collective-permute-done((bf16[1536,512]{1,0:T(8,128)(2,1)}, bf16[1536,512]{1,0:T(8,128)(2,1)}, u32[]{:S(2)}, u32[]{:S(2)}) %collective-permute-start.10) | collective-permute-done | bytes 1572896 | tf_op jit(solution)/shard_map/ppermute | solution.py:379
  45.4 2.8 %collective-permute-start.11 = (bf16[1536,512]{1,0:T(8,128)(2,1)}, bf16[1536,512]{1,0:T(8,128)(2,1)}, u32[]{:S(2)}, u32[]{:S(2)}) collective-permute-start(bf16[1536,512]{1,0:T(8,128)(2,1)} %collective-permute-done.10.refs_14_), channel_id=1, source_target_pairs={{0,4},{4,0},{1,5},{5,1},{2,6},{6,2},{3,7},{7,3},{8,12},{12,8},{9,1... | collective-permute-start | bytes 4718600 | tf_op jit(solution)/shard_map/ppermute | solution.py:353
  48.3 0.0 collective-permute-done.7.refs_10_
  48.3 1.5 %collective-permute-start.8 = (bf16[1536,512]{1,0:T(8,128)(2,1)}, bf16[1536,512]{1,0:T(8,128)(2,1)}, u32[]{:S(2)}, u32[]{:S(2)}) collective-permute-start(bf16[1536,512]{1,0:T(8,128)(2,1)} %collective-permute-done.7.refs_10_), channel_id=1, source_target_pairs={{0,4},{4,0},{1,5},{5,1},{2,6},{6,2},{3,7},{7,3},{8,12},{12,8},{9,1... | collective-permute-start | bytes 4718600 | tf_op jit(solution)/shard_map/ppermute | solution.py:353
  49.7 0.0 copy-done.8
  49.7 0.6 broadcast_in_dim.23.gp_ref
  50.3 0.0 copy-done.9
  50.3 0.6 broadcast_in_dim.24.gr_ref
  50.9 0.0 all-to-all-done
  50.9 2.3 %norm.1 = (bf16[4,392,128]{2,1,0:T(8,128)(2,1)}, bf16[4,392,128]{2,1,0:T(8,128)(2,1)}) custom-call(bf16[8,4,104,128]{3,2,1,0:T(8,128)(2,1)} %bitcast.17.in_ref, bf16[1,1536]{1,0:T(2,128)(2,1)} %broadcast_in_dim.23.gp_ref, bf16[1,1536]{1,0:T(2,128)(2,1)} %broadcast_in_dim.24.gr_ref), custom_call_target="tpu_custom_call" | custom-call | tf_op jit(solution)/shard_map/norm/pallas_call | solution.py:420
  53.3 1.3 collective-permute-start
  54.6 0.0 collective-permute-done.6.refs_3_.refs_5_.refs_9_
  54.6 1.5 %collective-permute-start.3 = (bf16[4,392,128]{2,1,0:T(8,128)(2,1)}, bf16[4,392,128]{2,1,0:T(8,128)(2,1)}, u32[]{:S(2)}, u32[]{:S(2)}) collective-permute-start(bf16[4,392,128]{2,1,0:T(8,128)(2,1)} %get-tuple-element.12.refs_1_), channel_id=1, source_target_pairs={{0,192},{64,0},{128,64},{192,128},{1,193},{65,1},{129,65},{193,129... | collective-permute-start | bytes 1204232 | tf_op jit(solution)/shard_map/ppermute | solution.py:353
  56.1 0.0 collective-permute-done.9.refs_5_.refs_7_.refs_13_
  56.1 0.0 collective-permute-start.1
  56.1 9.6 %collective-permute-done.refs_0_.refs_2_ = bf16[4,392,128]{2,1,0:T(8,128)(2,1)S(1)} collective-permute-done((bf16[4,392,128]{2,1,0:T(8,128)(2,1)}, bf16[4,392,128]{2,1,0:T(8,128)(2,1)S(1)}, u32[]{:S(2)}, u32[]{:S(2)}) %collective-permute-start) | collective-permute-done | bytes 401440 | tf_op jit(solution)/shard_map/ppermute | solution.py:353
  65.7 1.5 %collective-permute-start.2 = (bf16[4,392,128]{2,1,0:T(8,128)(2,1)}, bf16[4,392,128]{2,1,0:T(8,128)(2,1)}, u32[]{:S(2)}, u32[]{:S(2)}) collective-permute-start(bf16[4,392,128]{2,1,0:T(8,128)(2,1)} %get-tuple-element.11.refs_0_), channel_id=1, source_target_pairs={{0,192},{64,0},{128,64},{192,128},{1,193},{65,1},{129,65},{193,129... | collective-permute-start | bytes 1204232 | tf_op jit(solution)/shard_map/ppermute | solution.py:353
  67.2 0.0 collective-permute-done.3.refs_3_.refs_5_
  67.2 0.0 collective-permute-start.4
  67.2 7.1 %collective-permute-done.1.refs_1_.refs_3_ = bf16[4,392,128]{2,1,0:T(8,128)(2,1)S(1)} collective-permute-done((bf16[4,392,128]{2,1,0:T(8,128)(2,1)}, bf16[4,392,128]{2,1,0:T(8,128)(2,1)S(1)}, u32[]{:S(2)}, u32[]{:S(2)}) %collective-permute-start.1) | collective-permute-done | bytes 401440 | tf_op jit(solution)/shard_map/ppermute | solution.py:353
  74.3 0.0 copy-start.5
  74.3 0.7 copy-done.5
  75.0 1.5 %collective-permute-start.5 = (bf16[4,392,128]{2,1,0:T(8,128)(2,1)}, bf16[4,392,128]{2,1,0:T(8,128)(2,1)}, u32[]{:S(2)}, u32[]{:S(2)}) collective-permute-start(bf16[4,392,128]{2,1,0:T(8,128)(2,1)} %collective-permute-done.3.refs_3_.refs_5_), channel_id=1, source_target_pairs={{0,192},{64,0},{128,64},{192,128},{1,193},{65,1},{129,65},{193,129... | collective-permute-start | bytes 1204232 | tf_op jit(solution)/shard_map/ppermute | solution.py:353
  76.5 0.1 stack.64.base_ref
  76.6 0.0 copy-done.1
  76.6 0.0 copy-start.2
  76.6 1.0 copy-done.2
  77.6 0.0 copy-start.4
  77.6 1.0 copy-done.4
  78.6 0.0 copy-start.6
  78.6 3.9 %shard_map.122 = (f32[1,8,128]{2,1,0:T(8,128)S(1)}, bf16[2,128,1536]{2,1,0:T(8,128)(2,1)S(1)}) custom-call(s32[16]{0:T(128)S(1)} %stack.64.base_ref, bf16[4,392,128]{2,1,0:T(8,128)(2,1)S(1)} %copy-done.2, bf16[4,392,128]{2,1,0:T(8,128)(2,1)S(1)} %copy-done.4, bf16[1536,512]{1,0:T(8,128)(2,1)S(1)} %copy-done, ...), custom_call_target="tpu_custom_call" | custom-call | flops 805306368 | bytes 16777216 | tf_op jit(solution)/shard_map/pallas_call | solution.py:453
  82.6 0.0 copy-start.3
  82.6 0.0 collective-permute-done.2.refs_2_.refs_4_
  82.6 0.0 copy-done.6
  82.6 5.1 %shard_map.123 = (f32[2,8,128]{2,1,0:T(8,128)S(1)}, bf16[2,256,1536]{2,1,0:T(8,128)(2,1)S(1)}) custom-call(s32[16]{0:T(128)S(1)} %stack.64.base_ref, bf16[4,392,128]{2,1,0:T(8,128)(2,1)S(1)} %collective-permute-done.refs_0_.refs_2_, bf16[4,392,128]{2,1,0:T(8,128)(2,1)S(1)} %copy-done.6, bf16[4,392,128]{2,1,0:T(8,128)(2,1)} %collective-permute-done.2.refs_2_.refs_4_, ...), custom_call_target="tpu_custom_call" | custom-call | flops 1610612736 | bytes 16777216 | tf_op jit(solution)/shard_map/pallas_call | solution.py:453
  87.7 0.0 collective-permute-done.4.refs_6_
  87.7 0.0 collective-permute-done.5.refs_7_
  87.7 0.0 collective-permute-done.11.refs_15_
  87.7 0.0 collective-permute-done.8.refs_11_
  87.7 0.0 copy-done.3
  87.7 8.5 %logits_far.1 = f32[16,24,128]{2,1,0:T(8,128)S(1)} custom-call(s32[16]{0:T(128)S(1)} %stack.64.base_ref, bf16[4,392,128]{2,1,0:T(8,128)(2,1)S(1)} %copy-done.3, bf16[4,392,128]{2,1,0:T(8,128)(2,1)S(1)} %copy-done.4, bf16[4,392,128]{2,1,0:T(8,128)(2,1)S(1)} %collective-permute-done.refs_0_.refs_2_, bf16[4,392,128]{2,1,0:T(8,128)(2,1)S(1)} %copy-done.6, ...), custom_call_target="tpu_custom_call" | custom-call | flops 4026531840 | bytes 16777216 | tf_op jit(solution)/shard_map/logits_far/pallas_call | solution.py:473
  96.2 20.1 %all_to_all.15.in_ref = f32[16,24,128]{2,1,0:T(8,128)} all-to-all(f32[16,24,128]{2,1,0:T(8,128)S(1)} %logits_far.1), channel_id=1, replica_groups=mesh['y'=4,'z'=8,'c'=2,'xh'=2,'xl'=2] {'z','c'}, dimensions={0} | all-to-all | bytes 393216 | tf_op jit(solution)/shard_map/all_to_all | solution.py:494
  116.3 1.7 %merge.1 = f32[16,5,8,128]{3,2,1,0:T(8,128)} custom-call(f32[16,24,128]{2,1,0:T(8,128)} %all_to_all.15.in_ref), custom_call_target="tpu_custom_call" | custom-call | tf_op jit(solution)/shard_map/merge/pallas_call | solution.py:496
  118.0 3.5 %all-to-all-start.2 = ((f32[16,5,8,128]{3,2,1,0:T(8,128)}), f32[16,5,8,128]{3,2,1,0:T(8,128)S(1)}, u32[]{:S(2)}, u32[]{:S(2)}) async-start(f32[16,5,8,128]{3,2,1,0:T(8,128)} %merge.1), calls=%async_computation.2 | async-start | bytes 655360 | tf_op jit(solution)/shard_map/all_to_all | solution.py:503
  121.5 1.7 %tables.1.table_ref = f32[128,128]{1,0:T(8,128)} custom-call(s32[1]{0:T(128)} %bitcast.18.me_ref, s32[1,128]{1,0:T(1,128)} %bitcast.27, s32[1,128]{1,0:T(1,128)} %bitcast.28, f32[1,128]{1,0:T(1,128)} %bitcast.29), custom_call_target="tpu_custom_call" | custom-call | tf_op jit(solution)/shard_map/tables/pallas_call | solution.py:432
  123.2 7.7 %all-to-all-done.2.in_ref = f32[16,5,8,128]{3,2,1,0:T(8,128)S(1)} async-done(((f32[16,5,8,128]{3,2,1,0:T(8,128)}), f32[16,5,8,128]{3,2,1,0:T(8,128)S(1)}, u32[]{:S(2)}, u32[]{:S(2)}) %all-to-all-start.2) | async-done | bytes 327712 | tf_op jit(solution)/shard_map/all_to_all | solution.py:503
  130.9 0.0 copy-start.7
  130.9 0.7 copy-done.7
  131.6 2.1 %docs.1 = (f32[1,128]{1,0:T(1,128)}, f32[1,2]{1,0:T(1,128)}) custom-call(f32[16,5,8,128]{3,2,1,0:T(8,128)} %copy-done.7, f32[128,128]{1,0:T(8,128)} %tables.1.table_ref), custom_call_target="tpu_custom_call" | custom-call | tf_op jit(solution)/shard_map/docs/pallas_call | solution.py:504
Async XLA Ops:
  0.6 15.5 %copy-start = (bf16[1536,512]{1,0:T(8,128)(2,1)S(1)}, bf16[1536,512]{1,0:T(8,128)(2,1)}, u32[]{:S(2)}) copy-start(bf16[1536,512]{1,0:T(8,128)(2,1)} %refs_8_.1) | copy-start | bytes 4718596
  0.6 49.1 %copy-start.8 = (bf16[1536]{0:T(1024)(128)(2,1)S(1)}, bf16[1536]{0:T(1024)(128)(2,1)}, u32[]{:S(2)}) copy-start(bf16[1536]{0:T(1024)(128)(2,1)} %param.13) | copy-start | bytes 9220
  0.7 49.7 %copy-start.9 = (bf16[1536]{0:T(1024)(128)(2,1)S(1)}, bf16[1536]{0:T(1024)(128)(2,1)}, u32[]{:S(2)}) copy-start(bf16[1536]{0:T(1024)(128)(2,1)} %param.14) | copy-start | bytes 9220
  0.7 44.8 %collective-permute-start.10 = (bf16[1536,512]{1,0:T(8,128)(2,1)}, bf16[1536,512]{1,0:T(8,128)(2,1)}, u32[]{:S(2)}, u32[]{:S(2)}) collective-permute-start(bf16[1536,512]{1,0:T(8,128)(2,1)} %refs_12_.1), channel_id=1, source_target_pairs={{0,3},{1,2},{2,1},{3,0},{4,7},{5,6},{6,5},{7,4},{8,11},{9,10},{10,... | collective-permute-start | bytes 4718600 | tf_op jit(solution)/shard_map/ppermute | solution.py:379
  4.0 44.2 %collective-permute-start.7 = (bf16[1536,512]{1,0:T(8,128)(2,1)}, bf16[1536,512]{1,0:T(8,128)(2,1)}, u32[]{:S(2)}, u32[]{:S(2)}) collective-permute-start(bf16[1536,512]{1,0:T(8,128)(2,1)} %refs_8_.1), channel_id=1, source_target_pairs={{0,1},{1,0},{2,3},{3,2},{4,5},{5,4},{6,7},{7,6},{8,9},{9,8},{10,11... | collective-permute-start | bytes 4718600 | tf_op jit(solution)/shard_map/ppermute | solution.py:378
  6.1 70.5 %copy-start.1 = (bf16[1536,512]{1,0:T(8,128)(2,1)S(1)}, bf16[1536,512]{1,0:T(8,128)(2,1)}, u32[]{:S(2)}) copy-start(bf16[1536,512]{1,0:T(8,128)(2,1)} %refs_12_.1) | copy-start | bytes 4718596
  6.1 44.9 %all-to-all-start = ((bf16[32,104,128]{2,1,0:T(8,128)(2,1)}), bf16[32,104,128]{2,1,0:T(8,128)(2,1)}, u32[]{:S(2)}, u32[]{:S(2)}) async-start(bf16[32,104,128]{2,1,0:T(8,128)(2,1)} %bitcast.24), calls=%async_computation | async-start | bytes 1703936 | tf_op jit(solution)/shard_map/all_to_all | solution.py:416
  16.1 38.5 %collective-permute-start.6 = (bf16[1536,512]{1,0:T(8,128)(2,1)S(1)}, bf16[1536,512]{1,0:T(8,128)(2,1)}, u32[]{:S(2)}, u32[]{:S(2)}) collective-permute-start(bf16[1536,512]{1,0:T(8,128)(2,1)S(1)} %copy-done), channel_id=1, source_target_pairs={{0,4},{4,0},{1,5},{5,1},{2,6},{6,2},{3,7},{7,3},{8,12},{12,8},{9,1... | collective-permute-start | bytes 4718600 | tf_op jit(solution)/shard_map/ppermute | solution.py:353
  17.7 38.4 %collective-permute-start.9 = (bf16[1536,512]{1,0:T(8,128)(2,1)}, bf16[1536,512]{1,0:T(8,128)(2,1)}, u32[]{:S(2)}, u32[]{:S(2)}) collective-permute-start(bf16[1536,512]{1,0:T(8,128)(2,1)} %refs_12_.1), channel_id=1, source_target_pairs={{0,4},{4,0},{1,5},{5,1},{2,6},{6,2},{3,7},{7,3},{8,12},{12,8},{9,1... | collective-permute-start | bytes 4718600 | tf_op jit(solution)/shard_map/ppermute | solution.py:353
  45.4 42.3 %collective-permute-start.11 = (bf16[1536,512]{1,0:T(8,128)(2,1)}, bf16[1536,512]{1,0:T(8,128)(2,1)}, u32[]{:S(2)}, u32[]{:S(2)}) collective-permute-start(bf16[1536,512]{1,0:T(8,128)(2,1)} %collective-permute-done.10.refs_14_), channel_id=1, source_target_pairs={{0,4},{4,0},{1,5},{5,1},{2,6},{6,2},{3,7},{7,3},{8,12},{12,8},{9,1... | collective-permute-start | bytes 4718600 | tf_op jit(solution)/shard_map/ppermute | solution.py:353
  48.3 39.4 %collective-permute-start.8 = (bf16[1536,512]{1,0:T(8,128)(2,1)}, bf16[1536,512]{1,0:T(8,128)(2,1)}, u32[]{:S(2)}, u32[]{:S(2)}) collective-permute-start(bf16[1536,512]{1,0:T(8,128)(2,1)} %collective-permute-done.7.refs_10_), channel_id=1, source_target_pairs={{0,4},{4,0},{1,5},{5,1},{2,6},{6,2},{3,7},{7,3},{8,12},{12,8},{9,1... | collective-permute-start | bytes 4718600 | tf_op jit(solution)/shard_map/ppermute | solution.py:353
  53.3 12.4 %collective-permute-start = (bf16[4,392,128]{2,1,0:T(8,128)(2,1)}, bf16[4,392,128]{2,1,0:T(8,128)(2,1)S(1)}, u32[]{:S(2)}, u32[]{:S(2)}) collective-permute-start(bf16[4,392,128]{2,1,0:T(8,128)(2,1)} %get-tuple-element.11.refs_0_), channel_id=1, source_target_pairs={{0,64},{64,128},{128,192},{192,0},{1,65},{65,129},{129,193},{193,1... | collective-permute-start | bytes 1204232 | tf_op jit(solution)/shard_map/ppermute | solution.py:353
  54.6 12.6 %collective-permute-start.3 = (bf16[4,392,128]{2,1,0:T(8,128)(2,1)}, bf16[4,392,128]{2,1,0:T(8,128)(2,1)}, u32[]{:S(2)}, u32[]{:S(2)}) collective-permute-start(bf16[4,392,128]{2,1,0:T(8,128)(2,1)} %get-tuple-element.12.refs_1_), channel_id=1, source_target_pairs={{0,192},{64,0},{128,64},{192,128},{1,193},{65,1},{129,65},{193,129... | collective-permute-start | bytes 1204232 | tf_op jit(solution)/shard_map/ppermute | solution.py:353
  56.1 18.2 %collective-permute-start.1 = (bf16[4,392,128]{2,1,0:T(8,128)(2,1)}, bf16[4,392,128]{2,1,0:T(8,128)(2,1)S(1)}, u32[]{:S(2)}, u32[]{:S(2)}) collective-permute-start(bf16[4,392,128]{2,1,0:T(8,128)(2,1)} %get-tuple-element.12.refs_1_), channel_id=1, source_target_pairs={{0,64},{64,128},{128,192},{192,0},{1,65},{65,129},{129,193},{193,1... | collective-permute-start | bytes 1204232 | tf_op jit(solution)/shard_map/ppermute | solution.py:353
  65.7 16.9 %collective-permute-start.2 = (bf16[4,392,128]{2,1,0:T(8,128)(2,1)}, bf16[4,392,128]{2,1,0:T(8,128)(2,1)}, u32[]{:S(2)}, u32[]{:S(2)}) collective-permute-start(bf16[4,392,128]{2,1,0:T(8,128)(2,1)} %get-tuple-element.11.refs_0_), channel_id=1, source_target_pairs={{0,192},{64,0},{128,64},{192,128},{1,193},{65,1},{129,65},{193,129... | collective-permute-start | bytes 1204232 | tf_op jit(solution)/shard_map/ppermute | solution.py:353
  67.2 20.5 %collective-permute-start.4 = (bf16[4,392,128]{2,1,0:T(8,128)(2,1)S(1)}, bf16[4,392,128]{2,1,0:T(8,128)(2,1)}, u32[]{:S(2)}, u32[]{:S(2)}) collective-permute-start(bf16[4,392,128]{2,1,0:T(8,128)(2,1)S(1)} %collective-permute-done.refs_0_.refs_2_), channel_id=1, source_target_pairs={{0,64},{64,128},{128,192},{192,0},{1,65},{65,129},{129,193},{193,1... | collective-permute-start | bytes 1204232 | tf_op jit(solution)/shard_map/ppermute | solution.py:353
  74.3 0.8 copy-start.5
  75.0 12.7 %collective-permute-start.5 = (bf16[4,392,128]{2,1,0:T(8,128)(2,1)}, bf16[4,392,128]{2,1,0:T(8,128)(2,1)}, u32[]{:S(2)}, u32[]{:S(2)}) collective-permute-start(bf16[4,392,128]{2,1,0:T(8,128)(2,1)} %collective-permute-done.3.refs_3_.refs_5_), channel_id=1, source_target_pairs={{0,192},{64,0},{128,64},{192,128},{1,193},{65,1},{129,65},{193,129... | collective-permute-start | bytes 1204232 | tf_op jit(solution)/shard_map/ppermute | solution.py:353
  76.6 1.0 copy-start.2
  77.6 1.0 copy-start.4
  78.6 4.0 %copy-start.6 = (bf16[4,392,128]{2,1,0:T(8,128)(2,1)S(1)}, bf16[4,392,128]{2,1,0:T(8,128)(2,1)}, u32[]{:S(2)}) copy-start(bf16[4,392,128]{2,1,0:T(8,128)(2,1)} %copy-done.5) | copy-start | bytes 1204228
  82.6 5.2 %copy-start.3 = (bf16[4,392,128]{2,1,0:T(8,128)(2,1)S(1)}, bf16[4,392,128]{2,1,0:T(8,128)(2,1)}, u32[]{:S(2)}) copy-start(bf16[4,392,128]{2,1,0:T(8,128)(2,1)} %get-tuple-element.11.refs_0_) | copy-start | bytes 1204228
  118.0 12.9 %all-to-all-start.2 = ((f32[16,5,8,128]{3,2,1,0:T(8,128)}), f32[16,5,8,128]{3,2,1,0:T(8,128)S(1)}, u32[]{:S(2)}, u32[]{:S(2)}) async-start(f32[16,5,8,128]{3,2,1,0:T(8,128)} %merge.1), calls=%async_computation.2 | async-start | bytes 655360 | tf_op jit(solution)/shard_map/all_to_all | solution.py:503
  130.9 0.7 copy-start.7
